TPU v7x, 256 devices: a whole 4x4x8 slice. The times are simulated.
256 devices in a mesh: grid: 32 (over z, y), atom: 8 (over x, core).
Axes of the slice: x: 4, y: 4, z: 8, core: 2. Of those that a mesh axis runs over, the one named last changes fastest.
Arguments:
- weights: float32 [4194304], P(('grid', 'atom')), may hold values from 0.25 to 4
- target: float32 [4194304], P(('grid', 'atom')), may hold values from -6 to 6
- coupling: float32 [4194304], P(('grid', 'atom')), may hold values from -0.9 to 0.9
- multipole_basis: float32 [25, 4194304], P(None, ('grid', 'atom')), may hold values from -6 to 6
- rho_hist: float32 [8, 4194304], P(None, ('grid', 'atom')), may hold values from -6 to 6
- res_hist: float32 [8, 4194304], P(None, ('grid', 'atom')), may hold values from -6 to 6
- batch_atom: int32 [16384], P(('grid', 'atom')), may hold values from 0 to 4095
- owner_slot: int32 [4096], replicated, may hold values from 0 to 4095, each once
- slot_index: int32 [2], replicated, may hold values from 0 to 7
Outputs:
- density: float32 [4194304], P(('grid', 'atom'))
- moments: float32 [25, 4096], P(None, 'atom')
Inputs may be any that keep to these rules, and one draw needn't show every extreme that they name: `owner_slot`: each slot 0 to 4095 belongs to exactly one atom.
All inputs are finite; a program needn't handle non-finite values.
Results may differ from a plain program's by a relative error of at most 0.00011.
Values sent between devices are 32-bit elements; how exact they have to be, the bound alone decides.
A program may use at most 64 MiB of HBM per device.

v0:
```python
import math

import jax
import jax.numpy as jnp
import numpy as np
from jax import lax
from jax.sharding import Mesh
from jax.sharding import PartitionSpec as P

ITERS = 2
GRID_ATOM = ("grid_0", "grid_1", "atom_0", "atom_1")
ATOM = ("atom_0", "atom_1")
GRID = ("grid_0", "grid_1")


damping_table = np.array(
    [1.0 / (1 + degree) for degree in range(5) for order in range(2 * degree + 1)], dtype=np.float32
)
mixing_beta = 0.5
ridge_share = 0.1


def over_axes(value, axes):
    for axis in axes:
        value = lax.psum(value, axis)
    return value


def in_blocks(value, dim, peers):
    lengths = value.shape
    pieces = value.reshape(*lengths[:dim], peers, lengths[dim] // peers, *lengths[dim + 1 :])
    return jnp.moveaxis(pieces, dim, 0)


def sent_and_summed(value, axis, dim):
    peers = lax.axis_size(axis)
    pieces = lax.all_to_all(in_blocks(value, dim, peers), axis, 0, 0, tiled=True)
    return jnp.sum(pieces, axis=0)


def mixing_weights(intersect):
    hist_len = intersect.shape[0]
    ridge_val = ridge_share * jnp.trace(intersect) / hist_len
    shifted = intersect + ridge_val * jnp.eye(hist_len, dtype=intersect.dtype)
    factor = jnp.linalg.cholesky(shifted)
    forward = []
    for row_at in range(hist_len):
        entry_val = 1.0
        for col_at in range(row_at):
            entry_val = entry_val - factor[row_at, col_at] * forward[col_at]
        forward.append(entry_val / factor[row_at, row_at])
    backward = [None] * hist_len
    for row_at in reversed(range(hist_len)):
        entry_val = forward[row_at]
        for col_at in range(row_at + 1, hist_len):
            entry_val = entry_val - factor[col_at, row_at] * backward[col_at]
        backward[row_at] = entry_val / factor[row_at, row_at]
    solved = jnp.stack(backward)
    return solved / jnp.sum(solved)


def intersect_total(intersect_part):
    return over_axes(intersect_part, GRID_ATOM)


def moments_total(moment_part):
    owned_moms = sent_and_summed(moment_part, ATOM, 1)
    owned_moms = over_axes(owned_moms, GRID)
    all_moments = lax.all_gather(owned_moms, ATOM, axis=1, tiled=True)
    return (owned_moms, all_moments)


def local(
    weights,
    target,
    coupling,
    multipole_basis,
    rho_hist,
    res_hist,
    batch_atom,
    owner_slot,
    slot_index,
):
    hi_prec = lax.Precision.HIGHEST
    harmonics = multipole_basis.shape[0]
    points = weights.shape[0]
    batch_count = batch_atom.shape[0]
    batch_width = points // batch_count
    atom_total = owner_slot.shape[0]
    owned_count = atom_total // lax.axis_size(ATOM)
    atom_points = points * lax.axis_size(GRID) // owned_count
    moment_scale = 1.0 / math.sqrt(atom_points)
    damping = jnp.asarray(damping_table, dtype=weights.dtype)
    batch_slot = owner_slot[batch_atom]
    one_hot = (batch_slot[:, None] == jnp.arange(atom_total, dtype=jnp.int32)[None, :]).astype(
        weights.dtype
    )
    basis_blocks = multipole_basis.reshape(harmonics, batch_count, batch_width)
    intersect = None
    density = None
    owned_moms = None
    res_new = None
    previous = None
    for iteration in range(ITERS):
        fresh_start = iteration == 0
        if fresh_start:
            intersect_part = jnp.dot(res_hist * weights[None, :], res_hist.T, precision=hi_prec)
        else:
            intersect_part = jnp.dot(res_hist * weights[None, :], res_new, precision=hi_prec)
        if fresh_start:
            intersect = intersect_total(intersect_part)
        else:
            new_row = intersect_total(intersect_part)
            intersect = intersect.at[previous, :].set(new_row).at[:, previous].set(new_row)
        coeffs = mixing_weights(intersect)
        res_mix = jnp.dot(coeffs, res_hist, precision=hi_prec)
        fields = res_mix[None, :]
        leading = fields.shape[0]
        weighted = (fields * weights[None, :]).reshape(leading, 1, batch_count, batch_width)
        per_batch = jnp.sum(weighted * basis_blocks[None], axis=3)
        summed = jnp.dot(
            per_batch.reshape(leading * harmonics, batch_count), one_hot, precision=hi_prec
        )
        owned_moms, all_moments = moments_total(
            (summed.reshape(leading, harmonics, atom_total) * moment_scale)[0]
        )
        rho_mix = jnp.dot(coeffs, rho_hist, precision=hi_prec)
        at_batch = jnp.dot(all_moments * damping[:, None], one_hot.T, precision=hi_prec)
        density = rho_mix + mixing_beta * (
            res_mix - jnp.sum(at_batch[:, :, None] * basis_blocks, axis=0).reshape(points)
        )
        res_new = target + coupling * jnp.tanh(density) - density
        previous = slot_index[iteration]
        rho_hist = rho_hist.at[previous].set(density)
        res_hist = res_hist.at[previous].set(res_new)
    return (density, owned_moms)


def solution(mesh):
    torus = Mesh(mesh.devices.reshape(8, 4, 4, 2), ("grid_0", "grid_1", "atom_0", "atom_1"))
    placed = (
        P(GRID_ATOM),
        P(GRID_ATOM),
        P(GRID_ATOM),
        P(None, GRID_ATOM),
        P(None, GRID_ATOM),
        P(None, GRID_ATOM),
        P(GRID_ATOM),
        P(),
        P(),
    )
    return jax.shard_map(
        local, mesh=torus, in_specs=placed, out_specs=(P(GRID_ATOM), P(None, ATOM)), check_vma=False
    )
```

profile of v0, /device:TPU:2, one launch (start us, length us, event | category | flops | bytes accessed | tf_op | source)
XLA Modules:
  0.0 346.4 jit_solution(12972554845660243623)
XLA Ops:
  0.7 1.2 copy.43
  1.9 1.0 copy.42
  2.9 1.2 fusion.4
  4.1 20.0 %psum.84 = f32[8,8]{0,1:T(8,128)S(1)} all-reduce(f32[8,8]{0,1:T(8,128)S(1)} %fusion.4), channel_id=1, replica_groups=mesh['grid_0'=8,'grid_1'=4,'atom_0'=4,'atom_1'=2] {'grid_0'}, use_global_device_ids=true, to_apply=%region_0.0 | all-reduce | flops 64 | bytes 512 | tf_op jit(solution)/shard_map/psum | solution.py:25
  24.1 10.7 %psum.85 = f32[8,8]{0,1:T(8,128)S(1)} all-reduce(f32[8,8]{0,1:T(8,128)S(1)} %psum.84), channel_id=1, replica_groups=mesh['grid_0'=8,'grid_1'=4,'atom_0'=4,'atom_1'=2] {'grid_1'}, use_global_device_ids=true, to_apply=%region_1.0 | all-reduce | flops 64 | bytes 512 | tf_op jit(solution)/shard_map/psum | solution.py:25
  34.9 8.6 %psum.86 = f32[8,8]{0,1:T(8,128)S(1)} all-reduce(f32[8,8]{0,1:T(8,128)S(1)} %psum.85), channel_id=1, replica_groups=mesh['grid_0'=8,'grid_1'=4,'atom_0'=4,'atom_1'=2] {'atom_0'}, use_global_device_ids=true, to_apply=%region_2.0 | all-reduce | flops 64 | bytes 512 | tf_op jit(solution)/shard_map/psum | solution.py:25
  43.5 2.5 psum.87
  47.3 0.7 cholesky.44
  48.1 0.6 compare_reduce_fusion.1
  48.7 0.6 fusion.21
  49.4 0.7 fusion.33
  50.1 0.7 fusion.32
  97.3 0.6 copy.27
  98.0 1.3 copy-done.2
  99.7 0.8 gather_fusion
  101.4 1.1 copy.35
  102.4 6.4 %all-to-all-start = ((f32[8,25,512]{2,1,0:T(8,128)}), f32[8,25,512]{2,1,0:T(8,128)}, u32[]{:S(2)}, u32[]{:S(2)}) async-start(f32[8,25,512]{2,1,0:T(8,128)} %bitcast.166), calls=%async_computation | async-start | bytes 1048576 | tf_op jit(solution)/shard_map/all_to_all | solution.py:37
  109.0 0.7 and_reduce_fusion.1
  110.2 7.6 %all-to-all-done = f32[8,25,512]{2,1,0:T(8,128)} async-done(((f32[8,25,512]{2,1,0:T(8,128)}), f32[8,25,512]{2,1,0:T(8,128)}, u32[]{:S(2)}, u32[]{:S(2)}) %all-to-all-start) | async-done | bytes 409632 | tf_op jit(solution)/shard_map/all_to_all | solution.py:37
  117.8 1.1 reduce_sum.129
  118.9 27.4 %psum.88 = f32[25,512]{1,0:T(8,128)S(1)} all-reduce(f32[25,512]{1,0:T(8,128)S(1)} %reduce_sum.129), channel_id=1, replica_groups=mesh['grid_0'=8,'grid_1'=4,'atom_0'=4,'atom_1'=2] {'grid_0'}, use_global_device_ids=true, to_apply=%region_10.12 | all-reduce | flops 12800 | bytes 102400 | tf_op jit(solution)/shard_map/psum | solution.py:25
  146.3 14.8 %psum.89 = f32[25,512]{1,0:T(8,128)S(1)} all-reduce(f32[25,512]{1,0:T(8,128)S(1)} %psum.88), channel_id=1, replica_groups=mesh['grid_0'=8,'grid_1'=4,'atom_0'=4,'atom_1'=2] {'grid_1'}, use_global_device_ids=true, to_apply=%region_11.13 | all-reduce | flops 12800 | bytes 102400 | tf_op jit(solution)/shard_map/psum | solution.py:25
  161.2 12.5 %all_gather.6 = f32[25,4096]{1,0:T(8,128)S(1)} all-gather(f32[25,512]{1,0:T(8,128)S(1)} %psum.89), channel_id=1, replica_groups=mesh['grid_0'=8,'grid_1'=4,'atom_0'=4,'atom_1'=2] {'atom_0','atom_1'}, dimensions={1}, use_global_device_ids=true | all-gather | bytes 460800 | tf_op jit(solution)/shard_map/all_gather | solution.py:69
  173.7 0.7 fusion.3
  174.9 1.2 copy.29
  177.0 0.8 broadcast_select_fusion
  178.3 1.2 convolution_bitcast_fusion
  179.6 16.1 %psum.90 = f32[8]{0:T(128)S(1)} all-reduce(f32[8]{0:T(128)S(1)} %convolution_bitcast_fusion), channel_id=1, replica_groups=mesh['grid_0'=8,'grid_1'=4,'atom_0'=4,'atom_1'=2] {'grid_0'}, use_global_device_ids=true, to_apply=%region_13.15 | all-reduce | flops 8 | bytes 64 | tf_op jit(solution)/shard_map/psum | solution.py:25
  195.7 9.7 %psum.91 = f32[8]{0:T(128)S(1)} all-reduce(f32[8]{0:T(128)S(1)} %psum.90), channel_id=1, replica_groups=mesh['grid_0'=8,'grid_1'=4,'atom_0'=4,'atom_1'=2] {'grid_1'}, use_global_device_ids=true, to_apply=%region_14.16 | all-reduce | flops 8 | bytes 64 | tf_op jit(solution)/shard_map/psum | solution.py:25
  205.3 9.8 %psum.92 = f32[8]{0:T(128)S(1)} all-reduce(f32[8]{0:T(128)S(1)} %psum.91), channel_id=1, replica_groups=mesh['grid_0'=8,'grid_1'=4,'atom_0'=4,'atom_1'=2] {'atom_0'}, use_global_device_ids=true, to_apply=%region_15.17 | all-reduce | flops 8 | bytes 64 | tf_op jit(solution)/shard_map/psum | solution.py:25
  215.1 0.7 and_reduce_fusion
  215.8 2.4 psum.93
  218.4 0.7 dynamic-slice_select_fusion
  221.3 0.7 cholesky.55
  222.1 0.6 compare_reduce_fusion
  222.7 0.6 select_select_fusion
  223.4 0.7 fusion.31
  224.1 0.7 fusion.30
  270.9 1.7 fusion.1
  273.5 1.0 copy.34
  274.5 4.6 %all-to-all-start.1 = ((f32[8,25,512]{2,1,0:T(8,128)}), f32[8,25,512]{2,1,0:T(8,128)S(1)}, u32[]{:S(2)}, u32[]{:S(2)}) async-start(f32[8,25,512]{2,1,0:T(8,128)} %bitcast.156), calls=%async_computation.1 | async-start | bytes 1048576 | tf_op jit(solution)/shard_map/all_to_all | solution.py:37
  280.1 7.8 %all-to-all-done.1 = f32[8,25,512]{2,1,0:T(8,128)S(1)} async-done(((f32[8,25,512]{2,1,0:T(8,128)}), f32[8,25,512]{2,1,0:T(8,128)S(1)}, u32[]{:S(2)}, u32[]{:S(2)}) %all-to-all-start.1) | async-done | bytes 409632 | tf_op jit(solution)/shard_map/all_to_all | solution.py:37
  288.0 27.4 %psum.94 = f32[25,512]{1,0:T(8,128)S(1)} all-reduce(f32[25,512]{1,0:T(8,128)S(1)} %reduce_sum.140), channel_id=1, replica_groups=mesh['grid_0'=8,'grid_1'=4,'atom_0'=4,'atom_1'=2] {'grid_0'}, use_global_device_ids=true, to_apply=%region_21.23 | all-reduce | flops 12800 | bytes 102400 | tf_op jit(solution)/shard_map/psum | solution.py:25
  315.5 14.8 %psum.95 = f32[25,512]{1,0:T(8,128)S(1)} all-reduce(f32[25,512]{1,0:T(8,128)S(1)} %psum.94), channel_id=1, replica_groups=mesh['grid_0'=8,'grid_1'=4,'atom_0'=4,'atom_1'=2] {'grid_1'}, use_global_device_ids=true, to_apply=%region_22.24 | all-reduce | flops 12800 | bytes 102400 | tf_op jit(solution)/shard_map/psum | solution.py:25
  330.3 12.5 %all_gather.7 = f32[25,4096]{1,0:T(8,128)S(1)} all-gather(f32[25,512]{1,0:T(8,128)S(1)} %psum.95), channel_id=1, replica_groups=mesh['grid_0'=8,'grid_1'=4,'atom_0'=4,'atom_1'=2] {'atom_0','atom_1'}, dimensions={1}, use_global_device_ids=true | all-gather | bytes 460800 | tf_op jit(solution)/shard_map/all_gather | solution.py:69
  342.8 0.7 fusion.2
  344.0 1.2 copy.31
  345.7 0.6 multiply_add_fusion
  (64 shorter events, 10.3 us)
Async XLA Ops:
  0.6 99.0 %copy-start = (s32[4096]{0:T(1024)S(1)}, s32[4096]{0:T(1024)}, u32[]{:S(2)}) copy-start(s32[4096]{0:T(1024)} %param.26) | copy-start | bytes 49156
  0.6 2.3 copy-start.3
  0.7 96.7 %copy-start.1 = (f32[25,16384]{1,0:T(8,128)S(1)}, f32[25,16384]{1,0:T(8,128)}, u32[]{:S(2)}) copy-start(f32[25,16384]{1,0:T(8,128)} %param.22) | copy-start | bytes 4915204
  97.3 0.7 copy-start.10
  98.0 1.4 copy-start.2
  100.4 8.4 %copy-start.8 = (s32[2]{0:T(128)S(1)}, s32[2]{0:T(128)}, u32[]{:S(2)}) copy-start(s32[2]{0:T(128)} %param.27) | copy-start | bytes 28
  100.4 8.5 %copy-start.9 = (s32[2]{0:T(128)S(1)}, s32[2]{0:T(128)}, u32[]{:S(2)}) copy-start(s32[2]{0:T(128)} %constant.135.clone.1) | copy-start | bytes 28
  101.3 72.3 %copy-start.7 = (f32[25]{0:T(128)S(1)}, f32[25]{0:T(128)}, u32[]{:S(2)}) copy-start(f32[25]{0:T(128)} %constant.143.clone) | copy-start | bytes 304
  102.4 15.4 %all-to-all-start = ((f32[8,25,512]{2,1,0:T(8,128)}), f32[8,25,512]{2,1,0:T(8,128)}, u32[]{:S(2)}, u32[]{:S(2)}) async-start(f32[8,25,512]{2,1,0:T(8,128)} %bitcast.166), calls=%async_computation | async-start | bytes 1048576 | tf_op jit(solution)/shard_map/all_to_all | solution.py:37
  176.1 0.8 copy-start.5
  176.1 0.9 copy-start.6
  274.5 13.4 %all-to-all-start.1 = ((f32[8,25,512]{2,1,0:T(8,128)}), f32[8,25,512]{2,1,0:T(8,128)S(1)}, u32[]{:S(2)}, u32[]{:S(2)}) async-start(f32[8,25,512]{2,1,0:T(8,128)} %bitcast.156), calls=%async_computation.1 | async-start | bytes 1048576 | tf_op jit(solution)/shard_map/all_to_all | solution.py:37
  330.3 13.7 %copy-start.4 = (f32[25,512]{1,0:T(8,128)}, f32[25,512]{1,0:T(8,128)S(1)}, u32[]{:S(2)}) copy-start(f32[25,512]{1,0:T(8,128)S(1)} %psum.95) | copy-start | bytes 153604
where the time goes:
time: 351 us; the launch traced here: 346 us
  blocking collectives  189 us (54%)
  between operations  93.7 us (27%)
  local copies, waits for them, and re-layouts  16.1 us (5%)
  waiting for transfers between devices  15.4 us (4%)
  other arithmetic  13.6 us (4%)
  starting transfers between devices  11 us (3%)
  matrix products  7.3 us (2%)
    psum x12, blocking collectives, over_axes(): value = lax.psum(value, axis)  164 us
    all_gather x2, blocking collectives, moments_total(): all_moments = lax.all_gather(owned_moms, ATOM, axis=1, tiled=True)  25 us
    all_to_all x2, waiting for transfers between devices, sent_and_summed(): lax.all_to_all(in_blocks(value, dim, peers), axis, 0, 0, tiled=True)  15.4 us
    all_to_all x2, starting transfers between devices, sent_and_summed(): lax.all_to_all(in_blocks(value, dim, peers), axis, 0, 0, tiled=True)  11 us
    unnamed x31, local copies, waits for them, and re-layouts  8.14 us
  transfers between devices with their start and end apart: 2, of which 2 were waited for; matrix products, arithmetic and copies ran while one was open for 1% of the time, Pallas kernels for 0%

commit v1 on v0

v1 whole, which is shorter than its diff:
```python
import functools
import math

import jax
import jax.numpy as jnp
import numpy as np
from jax import lax
from jax.experimental import pallas as pl
from jax.experimental.pallas import tpu as pltpu
from jax.sharding import PartitionSpec as P

H = 8
LM = 25
ITERS = 2
BETA = 0.5
RIDGE = 0.1
LANES = 128
NZ, NY, NX, NC = 8, 4, 4, 2
PLANE = NY * NX * NC
MESH = pl.DeviceIdType.MESH
F32 = jnp.float32
I32 = jnp.int32


def kernel(
    tiles, batches, scale,
    w_hbm, tgt_hbm, cpl_hbm, basis_hbm, rho_hbm, res_hbm, atom_sm, owner_sm, hist_sm,
    dens_out, mom_out,
    w, tgt, cpl, basis, rho, res,
    slot_send, slot_recv, irow_send, irow_recv, zrow_send, zrow_recv,
    raw_send, raw_recv, part_send, part_recv, back_send, back_recv, blk_send, blk_recv,
    onehot, xparts,
    load_sem,
    slot_ss, slot_rs, irow_ss, irow_rs, zrow_ss, zrow_rs,
    raw_ss, raw_rs, part_ss, part_rs, back_ss, back_rs, blk_ss, blk_rs,
):
    grid = lax.axis_index("grid")
    atom = lax.axis_index("atom")
    z, y = grid // NY, grid % NY
    x, c = atom // NC, atom % NC
    me = y * (NX * NC) + atom

    ys = [(y + d) % NY for d in range(NY)]
    xs = [(x + d) % NX for d in range(NX)]
    cs = [c, 1 - c]
    peers = []
    for dy in (2, 1, 3, 0):
        for dx in (2, 1, 3, 0):
            for dc in (1, 0):
                if dy or dx or dc:
                    pa = xs[dx] * NC + cs[dc]
                    peers.append((z * NY + ys[dy], pa, ys[dy] * (NX * NC) + pa))
    zpeers = []
    for dz in (4, 3, 5, 2, 6, 1, 7):
        pz = (z + dz) % NZ
        zpeers.append((pz * NY + y, atom, pz))
    ypeers = [(z * NY + ys[dy], atom, ys[dy]) for dy in (2, 1, 3)]

    barrier = pltpu.get_barrier_semaphore()
    for pg, pa, _ in peers + zpeers:
        pl.semaphore_signal(barrier, inc=1, device_id=(pg, pa), device_id_type=MESH)

    loads = [
        pltpu.make_async_copy(src, dst, load_sem.at[n])
        for n, (src, dst) in enumerate(
            [(w_hbm, w), (res_hbm, res), (basis_hbm, basis), (rho_hbm, rho), (tgt_hbm, tgt), (cpl_hbm, cpl)]
        )
    ]
    for load in loads:
        load.start()

    sub = lax.broadcasted_iota(I32, (8, LANES), 0)
    lane = lax.broadcasted_iota(I32, (8, LANES), 1)
    low = lane < 64

    def to_peers(targets, src, dst, slot, ssem, rsem, per_peer=False):
        copies = []
        for n, (pg, pa, pslot) in enumerate(targets):
            copy = pltpu.make_async_remote_copy(
                src_ref=src.at[pslot] if per_peer else src,
                dst_ref=dst.at[slot],
                send_sem=ssem.at[n],
                recv_sem=rsem.at[slot],
                device_id=(pg, pa),
                device_id_type=MESH,
            )
            copy.start()
            copies.append(copy)
        return copies

    def arrived(targets, src, dst, ssem, rsem, per_peer=False):
        for n, (pg, pa, pslot) in enumerate(targets):
            pltpu.make_async_remote_copy(
                src_ref=src.at[pslot] if per_peer else src,
                dst_ref=dst.at[pslot],
                send_sem=ssem.at[n],
                recv_sem=rsem.at[pslot],
                device_id=(pg, pa),
                device_id_type=MESH,
            ).wait_recv()

    def tree_sum(parts):
        parts = list(parts)
        while len(parts) > 1:
            parts = [a + b for a, b in zip(parts[::2], parts[1::2])] + ([parts[-1]] if len(parts) % 2 else [])
        return parts[0]

    def over_subs(v):
        v = v + pltpu.roll(v, 4, 0)
        v = v + pltpu.roll(v, 2, 0)
        return v + pltpu.roll(v, 1, 0)

    def tile_at(ref, at):
        return ref[:, pl.ds(pl.multiple_of(at * LANES, LANES), LANES)]

    def row_at(ref, at):
        return jnp.broadcast_to(ref[pl.ds(at, 1), :], (8, LANES))

    def basis_tile(kt, at):
        cols = pl.ds(pl.multiple_of(at * LANES, LANES), LANES)
        if kt < 3:
            return basis[pl.ds(kt * 8, 8), cols]
        return jnp.broadcast_to(basis[pl.ds(24, 1), cols], (8, LANES))

    def row_of(columns):
        total = jnp.zeros((8, LANES), F32)
        for d, column in enumerate(columns):
            total = jnp.where(lane == d * 8 + sub, column, total)
        return over_subs(total)

    sends = []

    def all_summed(row, it):
        irow_send[it] = row[0:1]
        sends.extend(to_peers(peers, irow_send.at[it], irow_recv.at[it], me, irow_ss.at[it], irow_rs.at[it]))
        return row

    def plane_sum(it):
        arrived(peers, irow_send.at[it], irow_recv.at[it], irow_ss.at[it], irow_rs.at[it])
        row = tree_sum([irow_send[it]] + [irow_recv[it, pslot] for _, _, pslot in peers])
        zrow_send[it] = row
        sends.extend(to_peers(zpeers, zrow_send.at[it], zrow_recv.at[it], z, zrow_ss.at[it], zrow_rs.at[it]))

    def slice_sum(it):
        arrived(zpeers, zrow_send.at[it], zrow_recv.at[it], zrow_ss.at[it], zrow_rs.at[it])
        row = tree_sum([zrow_send[it]] + [zrow_recv[it, pslot] for _, _, pslot in zpeers])
        return jnp.broadcast_to(row, (8, LANES))

    def mixing(total):
        def entry(i, j):
            d = (i - j) % 8
            at = d * 8 + i if d <= 4 else (8 - d) * 8 + j
            return jnp.broadcast_to(total[:, at : at + 1], (8, LANES))

        a = {(i, j): entry(i, j) for i in range(H) for j in range(i + 1)}
        ridge = RIDGE * tree_sum([a[i, i] for i in range(H)]) / H
        for i in range(H):
            a[i, i] = a[i, i] + ridge
        ones = jnp.ones((8, LANES), F32)
        rhs = [ones] * H
        inverse = []
        factor = {}
        for k in range(H):
            inv = 1.0 / a[k, k]
            inverse.append(inv)
            for i in range(k + 1, H):
                factor[i, k] = a[i, k] * inv
            for i in range(k + 1, H):
                for j in range(k + 1, i + 1):
                    a[i, j] = a[i, j] - factor[i, k] * a[j, k]
                rhs[i] = rhs[i] - factor[i, k] * rhs[k]
        solved = [None] * H
        for k in reversed(range(H)):
            value = rhs[k] * inverse[k]
            for i in range(k + 1, H):
                value = value - factor[i, k] * solved[i]
            solved[k] = value
        share = 1.0 / tree_sum(solved)
        column = solved[0]
        for i in range(1, H):
            column = jnp.where(sub == i, solved[i], column)
        return column * share

    def raw_moments(column):
        def step(b, accs):
            accs = list(accs)
            sums = [None] * 4
            for half in range(2):
                at = b * 2 + half
                wr = over_subs(tile_at(res, at) * column) * row_at(w, at)
                for kt in range(4):
                    part = basis_tile(kt, at) * wr
                    sums[kt] = part if half == 0 else sums[kt] + part
            here = lane == b
            return tuple(
                jnp.where(here, jnp.sum(sums[kt], axis=1, keepdims=True), accs[kt]) for kt in range(4)
            )

        zero = jnp.zeros((8, LANES), F32)
        return lax.fori_loop(0, batches, step, (zero,) * 4, unroll=4)

    def packed(t0, t1, t2, t3):
        first = jnp.where(low, t0, pltpu.roll(t1, 64, 1))
        second = jnp.where(
            sub < 4,
            jnp.where(low, t2, pltpu.roll(pltpu.roll(t2, 4, 0), 64, 1)),
            jnp.where((sub == 4) & low, pltpu.roll(t3, 4, 0), 0.0),
        )
        return first, second

    def unpacked(first, second):
        moved = pltpu.roll(second, 64, 1)
        t2 = jnp.where(sub < 4, second, pltpu.roll(moved, 4, 0))
        t3 = jnp.where(sub == 0, pltpu.roll(second, 4, 0), 0.0)
        return first, pltpu.roll(first, 64, 1), t2, t3

    def three(v):
        hi = v.astype(jnp.bfloat16)
        rest = v - hi.astype(F32)
        mid = rest.astype(jnp.bfloat16)
        lo = (rest - mid.astype(F32)).astype(jnp.bfloat16)
        return hi, mid, lo

    def pair_joined(a, b):
        return jnp.where(low, a, pltpu.roll(b, 64, 1)), jnp.where(low, pltpu.roll(a, 64, 1), b)

    def owner_partial(it):
        for pair in range(PLANE // 2):
            cols = pl.ds(pair * LANES, LANES)
            for half in range(2):
                rows = pl.ds(half * 8, 8)
                a, b = pair_joined(raw_recv[it, 2 * pair, rows, :], raw_recv[it, 2 * pair + 1, rows, :])
                both = jnp.concatenate([a, b], axis=0)
                for n, part in enumerate(three(both)):
                    xparts[pl.ds(n * 32 + half * 16, 16), cols] = part
        sums = lax.dot_general(xparts[...], onehot[...], (((1,), (1,)), ((), ())), preferred_element_type=F32)
        sums = sums[0:32] + sums[32:64] + sums[64:96]
        part_send[it, 0:16] = sums[0:16]
        part_send[it, 16:24] = jnp.where(sub < 4, sums[16:24], pltpu.roll(sums[24:32], 4, 0))
        part_send[it, 24:32] = jnp.where(sub < 1, pltpu.roll(sums[16:24], 4, 0), 0.0)

    def back_values(it, block):
        tiles_of = [block[kt * 8 : kt * 8 + 8] for kt in range(4)]
        degree = [lax.broadcasted_iota(I32, (8, LANES), 0) + kt * 8 for kt in range(4)]
        damped = []
        for kt in range(4):
            k = degree[kt]
            damp = jnp.where(k < 1, 1.0, jnp.where(k < 4, 1 / 2, jnp.where(k < 9, 1 / 3, jnp.where(k < 16, 1 / 4, 1 / 5))))
            damped.append(tiles_of[kt] * damp)
        low_rows = jnp.where(sub < 4, damped[2], jnp.where(sub == 4, pltpu.roll(damped[3], 4, 0), 0.0))
        high_rows = jnp.where(sub < 4, pltpu.roll(damped[2], 4, 0), 0.0)
        rows = jnp.concatenate([damped[0], damped[1], low_rows, high_rows], axis=0)
        picked = jnp.dot(jnp.concatenate(three(rows), axis=0), onehot[...], preferred_element_type=F32)
        picked = picked[0:32] + picked[32:64] + picked[64:96]
        for pair in range(PLANE // 2):
            cols = slice(pair * LANES, (pair + 1) * LANES)
            for half in range(2):
                a, b = pair_joined(picked[half * 16 : half * 16 + 8, cols], picked[half * 16 + 8 : half * 16 + 16, cols])
                back_send[it, 2 * pair, half * 8 : half * 8 + 8, :] = a
                back_send[it, 2 * pair + 1, half * 8 : half * 8 + 8, :] = b

    loads[0].wait()
    loads[1].wait()

    def products(step_at, accs):
        accs = list(accs)
        for u in range(4):
            at = step_at * 4 + u
            r = tile_at(res, at)
            wr = r * row_at(w, at)
            accs[0] = accs[0] + wr * r
            for d in range(1, 5):
                accs[d] = accs[d] + wr * pltpu.roll(r, d, 0)
        return tuple(accs)

    accs = lax.fori_loop(0, tiles // 4, products, (jnp.zeros((8, LANES), F32),) * 5)
    first_row = row_of([jnp.sum(acc, axis=1, keepdims=True) for acc in accs])

    pl.semaphore_wait(barrier, len(peers) + len(zpeers))
    all_summed(first_row, 0)

    def slot_step(b, row):
        return jnp.where(lane == b, owner_sm[atom_sm[b]], row)

    slots = lax.fori_loop(0, batches, slot_step, jnp.full((8, LANES), -1, I32), unroll=4)
    slot_send[...] = slots[0:1]
    slot_recv[me] = slots[0:1]
    sends.extend(to_peers(peers, slot_send, slot_recv, me, slot_ss, slot_rs))
    for load in loads[2:]:
        load.wait()

    plane_sum(0)

    arrived(peers, slot_send, slot_recv, slot_ss, slot_rs)
    first_slot = atom * 512 + y * LANES
    for pair in range(PLANE // 2):
        left = jnp.broadcast_to(slot_recv[2 * pair], (8, LANES))
        right = jnp.broadcast_to(slot_recv[2 * pair + 1], (8, LANES))
        rel = jnp.where(low, left, pltpu.roll(right, 64, 1)) - first_slot
        for st in range(LANES // 16):
            halves = [jnp.where(rel == sub + (st * 16 + h * 8), 1.0, 0.0) for h in range(2)]
            onehot[pl.ds(st * 16, 16), pl.ds(pair * LANES, LANES)] = jnp.concatenate(halves, axis=0).astype(jnp.bfloat16)

    total = slice_sum(0)
    for it in range(ITERS):
        column = mixing(total)
        for rows, value in zip((pl.ds(0, 8), pl.ds(8, 8)), packed(*raw_moments(column))):
            raw_send[it, rows, :] = value
            raw_recv[it, me, rows, :] = value
        sends.extend(to_peers(peers, raw_send.at[it], raw_recv.at[it], me, raw_ss.at[it], raw_rs.at[it]))
        arrived(peers, raw_send.at[it], raw_recv.at[it], raw_ss.at[it], raw_rs.at[it])
        owner_partial(it)
        sends.extend(to_peers(zpeers, part_send.at[it], part_recv.at[it], z, part_ss.at[it], part_rs.at[it]))
        arrived(zpeers, part_send.at[it], part_recv.at[it], part_ss.at[it], part_rs.at[it])
        block = tree_sum([part_send[it]] + [part_recv[it, pslot] for _, _, pslot in zpeers]) * scale
        if it == ITERS - 1:
            blk_send[...] = block
            sends.extend(to_peers(ypeers, blk_send, blk_recv, y, blk_ss, blk_rs))
            blk_recv[y] = block
        back_values(it, block)
        sends.extend(
            to_peers(peers, back_send.at[it], back_recv.at[it], me, back_ss.at[it], back_rs.at[it], per_peer=True)
        )
        arrived(peers, back_send.at[it], back_recv.at[it], back_ss.at[it], back_rs.at[it], per_peer=True)
        mine = tree_sum([back_send[it, me]] + [back_recv[it, pslot] for _, _, pslot in peers]) * BETA
        at_batch = unpacked(mine[0:8], mine[8:16])
        hist_at = hist_sm[it]

        def density_step(group, carry):
            at_tiles, acc = carry
            for u in range(8):
                spread = [jnp.broadcast_to(t[:, u : u + 1], (8, LANES)) for t in at_tiles]
                for half in range(2):
                    at = (group * 8 + u) * 2 + half
                    cols = pl.ds(pl.multiple_of(at * LANES, LANES), LANES)
                    r, q = res[:, cols], rho[:, cols]
                    v = column * (q + BETA * r)
                    corr = tree_sum([basis_tile(kt, at) * spread[kt] for kt in range(4)])
                    dens = over_subs(v - corr)
                    if it == ITERS - 1:
                        dens_out[pl.ds(at, 1), :] = dens[0:1]
                    else:
                        new = row_at(tgt, at) + row_at(cpl, at) * jnp.tanh(dens) - dens
                        r = jnp.where(sub == hist_at, new, r)
                        res[:, cols] = r
                        rho[:, cols] = jnp.where(sub == hist_at, dens, q)
                        acc = acc + r * (new * row_at(w, at))
            return tuple(pltpu.roll(t, LANES - 8, 1) for t in at_tiles), acc

        _, acc = lax.fori_loop(0, batches // 8, density_step, (at_batch, jnp.zeros((8, LANES), F32)))
        if it < ITERS - 1:
            mine_new = jnp.broadcast_to(jnp.sum(acc, axis=1, keepdims=True), (8, LANES))
            columns = [
                jnp.where(sub == hist_at, pltpu.roll(mine_new, d, 0) if d else mine_new, mine_new) for d in range(5)
            ]
            all_summed(row_of(columns), it + 1)
            plane_sum(it + 1)
            row_i = lane % 8
            row_j = (row_i - lane // 8 + 8) % 8
            total = jnp.where((row_i == hist_at) | (row_j == hist_at), slice_sum(it + 1), total)

    arrived(ypeers, blk_send, blk_recv, blk_ss, blk_rs)
    for q in range(NY):
        mom_out[:, q * LANES : (q + 1) * LANES] = blk_recv[q, 0:LM]
    for copy in sends:
        copy.wait_send()


def local(weights, target, coupling, multipole_basis, rho_hist, res_hist, batch_atom, owner_slot, slot_index):
    points = weights.shape[0]
    batches = batch_atom.shape[0]
    tiles = points // LANES
    slots = owner_slot.shape[0]
    owned = slots // lax.axis_size("atom")
    scale = 1.0 / math.sqrt(points * lax.axis_size("grid") // owned)
    square = lambda v: v.reshape(tiles, LANES)
    vm, dma = pltpu.VMEM, pltpu.SemaphoreType.DMA
    anywhere = pl.BlockSpec(memory_space=pl.ANY)
    smem = pl.BlockSpec(memory_space=pltpu.SMEM)
    vmem = pl.BlockSpec(memory_space=pltpu.VMEM)
    density, moments = pl.pallas_call(
        functools.partial(kernel, tiles, batches, scale),
        out_shape=(jax.ShapeDtypeStruct((tiles, LANES), F32), jax.ShapeDtypeStruct((LM, owned), F32)),
        in_specs=[anywhere] * 6 + [smem] * 3,
        out_specs=(vmem, vmem),
        scratch_shapes=[
            vm((tiles, LANES), F32), vm((tiles, LANES), F32), vm((tiles, LANES), F32),
            vm((LM, points), F32), vm((H, points), F32), vm((H, points), F32),
            vm((1, LANES), I32), vm((PLANE, 1, LANES), I32),
            vm((ITERS, 1, LANES), F32), vm((ITERS, PLANE, 1, LANES), F32),
            vm((ITERS, 1, LANES), F32), vm((ITERS, NZ, 1, LANES), F32),
            vm((ITERS, 16, LANES), F32), vm((ITERS, PLANE, 16, LANES), F32),
            vm((ITERS, 32, LANES), F32), vm((ITERS, NZ, 32, LANES), F32),
            vm((ITERS, PLANE, 16, LANES), F32), vm((ITERS, PLANE, 16, LANES), F32),
            vm((32, LANES), F32), vm((NY, 32, LANES), F32),
            vm((LANES, PLANE * 64), jnp.bfloat16), vm((96, PLANE * 64), jnp.bfloat16),
            dma((6,)),
            dma((31,)), dma((PLANE,)),
            dma((ITERS, 31)), dma((ITERS, PLANE)),
            dma((ITERS, 7)), dma((ITERS, NZ)),
            dma((ITERS, 31)), dma((ITERS, PLANE)),
            dma((ITERS, 7)), dma((ITERS, NZ)),
            dma((ITERS, 31)), dma((ITERS, PLANE)),
            dma((3,)), dma((NY,)),
        ],
        compiler_params=pltpu.CompilerParams(collective_id=0, has_side_effects=True),
    )(
        square(weights), square(target), square(coupling), multipole_basis, rho_hist, res_hist,
        batch_atom, owner_slot, slot_index,
    )
    return density.reshape(points), moments


def solution(mesh):
    both = ("grid", "atom")
    placed = (P(both), P(both), P(both), P(None, both), P(None, both), P(None, both), P(both), P(), P())
    return jax.shard_map(
        local, mesh=mesh, in_specs=placed, out_specs=(P(both), P(None, "atom")), check_vma=False
    )
```

time: 351 us -> 81.3 us (0.23)
  the two profiles are of different devices: /device:TPU:2 before, /device:TPU:1 now
where the time goes in v1:
time: 81.3 us; the launch traced here: 81.1 us
  Pallas kernels  77.5 us (95%)
  local copies, waits for them, and re-layouts  2.95 us (4%)
    pallas_call x1, Pallas kernels, local(): pl.pallas_call(functools.partial(kernel, tiles, batches, scale), out_shap...  77.5 us
    unnamed x2, local copies, waits for them, and re-layouts  2.95 us

profile of v1, /device:TPU:1, one launch (start us, length us, event | category | flops | bytes accessed | tf_op | source)
XLA Modules:
  0.0 81.1 jit_solution(12973231463299566332)
XLA Ops:
  0.6 77.5 %shard_map.104 = (f32[128,128]{1,0:T(8,128)}, f32[25,512]{1,0:T(8,128)}) custom-call(f32[128,128]{1,0:T(8,128)} %bitcast.4, f32[128,128]{1,0:T(8,128)} %bitcast.5, f32[128,128]{1,0:T(8,128)} %bitcast.6, f32[25,16384]{1,0:T(8,128)} %basis_hbm.1, f32[8,16384]{1,0:T(8,128)} %rho_hbm.1, f32[8,16384]{1,0:T(8,128)} %res_hbm.1, s32[64]{0:T(128)} %atom_sm.1, ...), custom_call_target="tpu_custom_call" | custom-call | tf_op jit(solution)/shard_map/pallas_call | solution.py:381
  78.1 1.5 %copy.13 = f32[16384]{0:T(1024)} copy(f32[16384]{0:T(1024)} %bitcast.7) | data formatting | bytes 131072
  79.6 1.5 %copy.14 = f32[25,512]{1,0:T(8,128)} copy(f32[25,512]{1,0:T(8,128)} %get-tuple-element.9) | data formatting | bytes 102400

commit v2 on v1

--- a/solution.py
+++ b/solution.py
@@ -24,14 +24,15 @@
 
 def kernel(
     tiles, batches, scale,
-    w_hbm, tgt_hbm, cpl_hbm, basis_hbm, rho_hbm, res_hbm, atom_sm, owner_sm, hist_sm,
+    w_hbm, tgt_hbm, cpl_hbm, basis_hbm, rho_hbm, res_hbm, atom_hbm, owner_hbm, hist_hbm,
     dens_out, mom_out,
-    w, tgt, cpl, basis, rho, res,
-    slot_send, slot_recv, irow_send, irow_recv, zrow_send, zrow_recv,
+    w, tgt, cpl, basis, rho, res, fresh, weighted, merged, hist_moms,
+    atom_sm, owner_sm, hist_sm,
+    slot_send, slot_recv, zslot_recv, irow_send, irow_recv, zrow_send, zrow_recv,
     raw_send, raw_recv, part_send, part_recv, back_send, back_recv, blk_send, blk_recv,
-    onehot, xparts,
+    match, xparts,
     load_sem,
-    slot_ss, slot_rs, irow_ss, irow_rs, zrow_ss, zrow_rs,
+    slot_ss, slot_rs, zslot_ss, zslot_rs, irow_ss, irow_rs, zrow_ss, zrow_rs,
     raw_ss, raw_rs, part_ss, part_rs, back_ss, back_rs, blk_ss, blk_rs,
 ):
     grid = lax.axis_index("grid")
@@ -63,7 +64,10 @@
     loads = [
         pltpu.make_async_copy(src, dst, load_sem.at[n])
         for n, (src, dst) in enumerate(
-            [(w_hbm, w), (res_hbm, res), (basis_hbm, basis), (rho_hbm, rho), (tgt_hbm, tgt), (cpl_hbm, cpl)]
+            [
+                (w_hbm, w), (res_hbm, res), (basis_hbm, basis), (atom_hbm, atom_sm), (owner_hbm, owner_sm),
+                (hist_hbm, hist_sm), (rho_hbm, rho), (tgt_hbm, tgt), (cpl_hbm, cpl),
+            ]
         )
     ]
     for load in loads:
@@ -176,35 +180,78 @@
                 value = value - factor[i, k] * solved[i]
             solved[k] = value
         share = 1.0 / tree_sum(solved)
-        column = solved[0]
+        coeffs = [value * share for value in solved]
+        column = coeffs[0]
         for i in range(1, H):
-            column = jnp.where(sub == i, solved[i], column)
-        return column * share
-
-    def raw_moments(column):
-        def step(b, accs):
-            accs = list(accs)
-            sums = [None] * 4
-            for half in range(2):
-                at = b * 2 + half
-                wr = over_subs(tile_at(res, at) * column) * row_at(w, at)
-                for kt in range(4):
-                    part = basis_tile(kt, at) * wr
-                    sums[kt] = part if half == 0 else sums[kt] + part
-            here = lane == b
-            return tuple(
-                jnp.where(here, jnp.sum(sums[kt], axis=1, keepdims=True), accs[kt]) for kt in range(4)
-            )
-
-        zero = jnp.zeros((8, LANES), F32)
-        return lax.fori_loop(0, batches, step, (zero,) * 4, unroll=4)
+            column = jnp.where(sub == i, coeffs[i], column)
+        return coeffs, column
+
+    def merge(first, second, bit, axis):
+        clear = ((lane if axis == 1 else sub) & bit) == 0
+        return jnp.where(clear, first, second) + pltpu.roll(jnp.where(clear, second, first), bit, axis)
+
+    def merge_all(values, bit, axis):
+        while len(values) > 1:
+            values = [merge(p, q, bit, axis) for p, q in zip(values[::2], values[1::2])]
+            bit *= 2
+        return values[0]
+
+    def weigh(group):
+        for u in range(16):
+            at = group * 16 + u
+            wrow = row_at(w, at)
+            for kt in range(4):
+                weighted[u, kt] = basis_tile(kt, at) * wrow
+
+    def batch_sums(group, kt, field):
+        return merge_all([weighted[2 * u, kt] * field(2 * u) + weighted[2 * u + 1, kt] * field(2 * u + 1) for u in range(8)], 1, 1)
+
+    def joined(n):
+        total = merge_all([merged[g, n] for g in range(batches // 8)], 8, 1)
+        return total + pltpu.roll(total, 64, 1)
+
+    def history_moments():
+        def step(group, carry):
+            weigh(group)
+
+            def cols(u):
+                return pl.ds(pl.multiple_of((group * 16 + u) * LANES, LANES), LANES)
+
+            for i in range(H):
+                for kt in range(3):
+                    merged[group, i * 3 + kt] = batch_sums(
+                        group, kt, lambda u: jnp.broadcast_to(res[pl.ds(i, 1), cols(u)], (8, LANES))
+                    )
+            merged[group, 24] = batch_sums(group, 3, lambda u: res[:, cols(u)])
+            return carry
+
+        lax.fori_loop(0, batches // 8, step, 0)
+        for n in range(25):
+            hist_moms[n] = joined(n)
+
+    def fresh_moments(hist_at):
+        def step(group, carry):
+            weigh(group)
+            for kt in range(4):
+                merged[group, kt] = batch_sums(group, kt, lambda u: row_at(fresh, group * 16 + u))
+            return carry
+
+        lax.fori_loop(0, batches // 8, step, 0)
+        for kt in range(3):
+            value = joined(kt)
+            for i in range(H):
+                hist_moms[i * 3 + kt] = jnp.where(hist_at == i, value, hist_moms[i * 3 + kt])
+        hist_moms[24] = jnp.where(sub == hist_at, joined(3), hist_moms[24])
+
+    def raw_moments(coeffs, column):
+        return [tree_sum([coeffs[i] * hist_moms[i * 3 + kt] for i in range(H)]) for kt in range(3)] + [
+            over_subs(column * hist_moms[24])
+        ]
 
     def packed(t0, t1, t2, t3):
-        first = jnp.where(low, t0, pltpu.roll(t1, 64, 1))
+        first = jnp.where(low, t0, t1)
         second = jnp.where(
-            sub < 4,
-            jnp.where(low, t2, pltpu.roll(pltpu.roll(t2, 4, 0), 64, 1)),
-            jnp.where((sub == 4) & low, pltpu.roll(t3, 4, 0), 0.0),
+            sub < 4, jnp.where(low, t2, pltpu.roll(t2, 4, 0)), jnp.where((sub == 4) & low, t3, 0.0)
         )
         return first, second
 
@@ -224,7 +271,7 @@
     def pair_joined(a, b):
         return jnp.where(low, a, pltpu.roll(b, 64, 1)), jnp.where(low, pltpu.roll(a, 64, 1), b)
 
-    def owner_partial(it):
+    def gather_parts(it):
         for pair in range(PLANE // 2):
             cols = pl.ds(pair * LANES, LANES)
             for half in range(2):
@@ -233,31 +280,32 @@
                 both = jnp.concatenate([a, b], axis=0)
                 for n, part in enumerate(three(both)):
                     xparts[pl.ds(n * 32 + half * 16, 16), cols] = part
-        sums = lax.dot_general(xparts[...], onehot[...], (((1,), (1,)), ((), ())), preferred_element_type=F32)
-        sums = sums[0:32] + sums[32:64] + sums[64:96]
-        part_send[it, 0:16] = sums[0:16]
-        part_send[it, 16:24] = jnp.where(sub < 4, sums[16:24], pltpu.roll(sums[24:32], 4, 0))
-        part_send[it, 24:32] = jnp.where(sub < 1, pltpu.roll(sums[16:24], 4, 0), 0.0)
-
-    def back_values(it, block):
-        tiles_of = [block[kt * 8 : kt * 8 + 8] for kt in range(4)]
-        degree = [lax.broadcasted_iota(I32, (8, LANES), 0) + kt * 8 for kt in range(4)]
-        damped = []
-        for kt in range(4):
-            k = degree[kt]
-            damp = jnp.where(k < 1, 1.0, jnp.where(k < 4, 1 / 2, jnp.where(k < 9, 1 / 3, jnp.where(k < 16, 1 / 4, 1 / 5))))
-            damped.append(tiles_of[kt] * damp)
-        low_rows = jnp.where(sub < 4, damped[2], jnp.where(sub == 4, pltpu.roll(damped[3], 4, 0), 0.0))
-        high_rows = jnp.where(sub < 4, pltpu.roll(damped[2], 4, 0), 0.0)
-        rows = jnp.concatenate([damped[0], damped[1], low_rows, high_rows], axis=0)
-        picked = jnp.dot(jnp.concatenate(three(rows), axis=0), onehot[...], preferred_element_type=F32)
-        picked = picked[0:32] + picked[32:64] + picked[64:96]
-        for pair in range(PLANE // 2):
+
+    def matched(first_row, count):
+        sums = lax.dot_general(
+            xparts[...], match[pl.ds(first_row, count), :], (((1,), (1,)), ((), ())), preferred_element_type=F32
+        )
+        return sums[0:32] + sums[32:64] + sums[64:96]
+
+    def owner_partial():
+        sums = matched(NZ * 64, LANES)
+        part_send[0:16] = sums[0:16]
+        part_send[16:24] = jnp.where(sub < 4, sums[16:24], pltpu.roll(sums[24:32], 4, 0))
+        part_send[24:32] = jnp.where(sub < 1, pltpu.roll(sums[16:24], 4, 0), 0.0)
+
+    def peer_values(it):
+        picked = matched(0, NZ * 64)
+        for pair in range(NZ // 2):
             cols = slice(pair * LANES, (pair + 1) * LANES)
             for half in range(2):
                 a, b = pair_joined(picked[half * 16 : half * 16 + 8, cols], picked[half * 16 + 8 : half * 16 + 16, cols])
                 back_send[it, 2 * pair, half * 8 : half * 8 + 8, :] = a
                 back_send[it, 2 * pair + 1, half * 8 : half * 8 + 8, :] = b
+
+    def damped(kt, value):
+        k = sub + kt * 8
+        damp = jnp.where(k < 1, 1.0, jnp.where(k < 4, 1 / 2, jnp.where(k < 9, 1 / 3, jnp.where(k < 16, 1 / 4, 1 / 5))))
+        return value * (damp * (scale * BETA))
 
     loads[0].wait()
     loads[1].wait()
@@ -276,8 +324,10 @@
     accs = lax.fori_loop(0, tiles // 4, products, (jnp.zeros((8, LANES), F32),) * 5)
     first_row = row_of([jnp.sum(acc, axis=1, keepdims=True) for acc in accs])
 
-    pl.semaphore_wait(barrier, len(peers) + len(zpeers))
-    all_summed(first_row, 0)
+    loads[2].wait()
+    history_moments()
+    for load in loads[3:6]:
+        load.wait()
 
     def slot_step(b, row):
         return jnp.where(lane == b, owner_sm[atom_sm[b]], row)
@@ -285,75 +335,106 @@
     slots = lax.fori_loop(0, batches, slot_step, jnp.full((8, LANES), -1, I32), unroll=4)
     slot_send[...] = slots[0:1]
     slot_recv[me] = slots[0:1]
+    zslot_recv[z] = slots[0:1]
+
+    pl.semaphore_wait(barrier, len(peers) + len(zpeers))
+    all_summed(first_row, 0)
     sends.extend(to_peers(peers, slot_send, slot_recv, me, slot_ss, slot_rs))
-    for load in loads[2:]:
+    sends.extend(to_peers(zpeers, slot_send, zslot_recv, z, zslot_ss, zslot_rs))
+    for load in loads[6:]:
         load.wait()
 
     plane_sum(0)
 
     arrived(peers, slot_send, slot_recv, slot_ss, slot_rs)
+    arrived(zpeers, slot_send, zslot_recv, zslot_ss, zslot_rs)
     first_slot = atom * 512 + y * LANES
+    sources = []
     for pair in range(PLANE // 2):
         left = jnp.broadcast_to(slot_recv[2 * pair], (8, LANES))
         right = jnp.broadcast_to(slot_recv[2 * pair + 1], (8, LANES))
-        rel = jnp.where(low, left, pltpu.roll(right, 64, 1)) - first_slot
-        for st in range(LANES // 16):
-            halves = [jnp.where(rel == sub + (st * 16 + h * 8), 1.0, 0.0) for h in range(2)]
-            onehot[pl.ds(st * 16, 16), pl.ds(pair * LANES, LANES)] = jnp.concatenate(halves, axis=0).astype(jnp.bfloat16)
+        sources.append(jnp.where(low, left, pltpu.roll(right, 64, 1)))
+
+    def match_rows(at, wanted):
+        for pair in range(PLANE // 2):
+            halves = [jnp.where(sources[pair] == one, 1.0, 0.0) for one in wanted]
+            match[pl.ds(at, 16), pl.ds(pair * LANES, LANES)] = jnp.concatenate(halves, axis=0).astype(jnp.bfloat16)
+
+    def target_step(step_at, carry):
+        row = jnp.broadcast_to(zslot_recv[step_at // 4], (8, LANES)).astype(F32)
+        wanted = []
+        for h in range(2):
+            hit = lane == sub + ((step_at % 4) * 16 + h * 8)
+            column = jnp.sum(jnp.where(hit, row, 0.0), axis=1, keepdims=True)
+            wanted.append(jnp.broadcast_to(column, (8, LANES)).astype(I32))
+        match_rows(pl.multiple_of(step_at * 16, 16), wanted)
+        return carry
+
+    lax.fori_loop(0, NZ * 4, target_step, 0)
+    for st in range(LANES // 16):
+        match_rows(NZ * 64 + st * 16, [sub + (first_slot + st * 16 + h * 8) for h in range(2)])
 
     total = slice_sum(0)
     for it in range(ITERS):
-        column = mixing(total)
-        for rows, value in zip((pl.ds(0, 8), pl.ds(8, 8)), packed(*raw_moments(column))):
+        last = it == ITERS - 1
+        coeffs, column = mixing(total)
+        for rows, value in zip((pl.ds(0, 8), pl.ds(8, 8)), packed(*raw_moments(coeffs, column))):
             raw_send[it, rows, :] = value
             raw_recv[it, me, rows, :] = value
         sends.extend(to_peers(peers, raw_send.at[it], raw_recv.at[it], me, raw_ss.at[it], raw_rs.at[it]))
         arrived(peers, raw_send.at[it], raw_recv.at[it], raw_ss.at[it], raw_rs.at[it])
-        owner_partial(it)
-        sends.extend(to_peers(zpeers, part_send.at[it], part_recv.at[it], z, part_ss.at[it], part_rs.at[it]))
-        arrived(zpeers, part_send.at[it], part_recv.at[it], part_ss.at[it], part_rs.at[it])
-        block = tree_sum([part_send[it]] + [part_recv[it, pslot] for _, _, pslot in zpeers]) * scale
-        if it == ITERS - 1:
+        gather_parts(it)
+        if last:
+            owner_partial()
+            sends.extend(to_peers(zpeers, part_send, part_recv, z, part_ss, part_rs))
+        peer_values(it)
+        sends.extend(
+            to_peers(zpeers, back_send.at[it], back_recv.at[it], z, back_ss.at[it], back_rs.at[it], per_peer=True)
+        )
+        if last:
+            arrived(zpeers, part_send, part_recv, part_ss, part_rs)
+            block = tree_sum([part_send[...]] + [part_recv[pslot] for _, _, pslot in zpeers]) * scale
             blk_send[...] = block
             sends.extend(to_peers(ypeers, blk_send, blk_recv, y, blk_ss, blk_rs))
             blk_recv[y] = block
-        back_values(it, block)
-        sends.extend(
-            to_peers(peers, back_send.at[it], back_recv.at[it], me, back_ss.at[it], back_rs.at[it], per_peer=True)
-        )
-        arrived(peers, back_send.at[it], back_recv.at[it], back_ss.at[it], back_rs.at[it], per_peer=True)
-        mine = tree_sum([back_send[it, me]] + [back_recv[it, pslot] for _, _, pslot in peers]) * BETA
-        at_batch = unpacked(mine[0:8], mine[8:16])
+        arrived(zpeers, back_send.at[it], back_recv.at[it], back_ss.at[it], back_rs.at[it], per_peer=True)
+        mine = tree_sum([back_send[it, z]] + [back_recv[it, pslot] for _, _, pslot in zpeers])
+        at_batch = tuple(damped(kt, t) for kt, t in enumerate(unpacked(mine[0:8], mine[8:16])))
         hist_at = hist_sm[it]
 
         def density_step(group, carry):
             at_tiles, acc = carry
-            for u in range(8):
+            rows = pl.ds(pl.multiple_of(group * 8, 8), 8)
+            parts = []
+            for u in range(4):
                 spread = [jnp.broadcast_to(t[:, u : u + 1], (8, LANES)) for t in at_tiles]
                 for half in range(2):
-                    at = (group * 8 + u) * 2 + half
-                    cols = pl.ds(pl.multiple_of(at * LANES, LANES), LANES)
-                    r, q = res[:, cols], rho[:, cols]
-                    v = column * (q + BETA * r)
-                    corr = tree_sum([basis_tile(kt, at) * spread[kt] for kt in range(4)])
-                    dens = over_subs(v - corr)
-                    if it == ITERS - 1:
-                        dens_out[pl.ds(at, 1), :] = dens[0:1]
-                    else:
-                        new = row_at(tgt, at) + row_at(cpl, at) * jnp.tanh(dens) - dens
-                        r = jnp.where(sub == hist_at, new, r)
-                        res[:, cols] = r
-                        rho[:, cols] = jnp.where(sub == hist_at, dens, q)
-                        acc = acc + r * (new * row_at(w, at))
-            return tuple(pltpu.roll(t, LANES - 8, 1) for t in at_tiles), acc
-
-        _, acc = lax.fori_loop(0, batches // 8, density_step, (at_batch, jnp.zeros((8, LANES), F32)))
-        if it < ITERS - 1:
+                    at = group * 8 + u * 2 + half
+                    v = column * (tile_at(rho, at) + BETA * tile_at(res, at))
+                    parts.append(v - tree_sum([basis_tile(kt, at) * spread[kt] for kt in range(4)]))
+            dens = merge_all(parts, 1, 0)
+            if last:
+                dens_out[rows, :] = dens
+            else:
+                new = tgt[rows, :] + cpl[rows, :] * jnp.tanh(dens) - dens
+                fresh[rows, :] = new
+                weighed = new * w[rows, :]
+                for u in range(8):
+                    cols = pl.ds(pl.multiple_of((group * 8 + u) * LANES, LANES), LANES)
+                    r = jnp.where(sub == hist_at, jnp.broadcast_to(new[u : u + 1], (8, LANES)), res[:, cols])
+                    res[:, cols] = r
+                    rho[:, cols] = jnp.where(sub == hist_at, jnp.broadcast_to(dens[u : u + 1], (8, LANES)), rho[:, cols])
+                    acc = acc + r * jnp.broadcast_to(weighed[u : u + 1], (8, LANES))
+            return tuple(pltpu.roll(t, LANES - 4, 1) for t in at_tiles), acc
+
+        _, acc = lax.fori_loop(0, batches // 4, density_step, (at_batch, jnp.zeros((8, LANES), F32)))
+        if not last:
             mine_new = jnp.broadcast_to(jnp.sum(acc, axis=1, keepdims=True), (8, LANES))
             columns = [
                 jnp.where(sub == hist_at, pltpu.roll(mine_new, d, 0) if d else mine_new, mine_new) for d in range(5)
             ]
             all_summed(row_of(columns), it + 1)
+            fresh_moments(hist_at)
             plane_sum(it + 1)
             row_i = lane % 8
             row_j = (row_i - lane // 8 + 8) % 8
@@ -374,33 +455,35 @@
     owned = slots // lax.axis_size("atom")
     scale = 1.0 / math.sqrt(points * lax.axis_size("grid") // owned)
     square = lambda v: v.reshape(tiles, LANES)
-    vm, dma = pltpu.VMEM, pltpu.SemaphoreType.DMA
+    vm, sm, dma = pltpu.VMEM, pltpu.SMEM, pltpu.SemaphoreType.DMA
     anywhere = pl.BlockSpec(memory_space=pl.ANY)
-    smem = pl.BlockSpec(memory_space=pltpu.SMEM)
     vmem = pl.BlockSpec(memory_space=pltpu.VMEM)
     density, moments = pl.pallas_call(
         functools.partial(kernel, tiles, batches, scale),
         out_shape=(jax.ShapeDtypeStruct((tiles, LANES), F32), jax.ShapeDtypeStruct((LM, owned), F32)),
-        in_specs=[anywhere] * 6 + [smem] * 3,
+        in_specs=[anywhere] * 9,
         out_specs=(vmem, vmem),
         scratch_shapes=[
             vm((tiles, LANES), F32), vm((tiles, LANES), F32), vm((tiles, LANES), F32),
             vm((LM, points), F32), vm((H, points), F32), vm((H, points), F32),
-            vm((1, LANES), I32), vm((PLANE, 1, LANES), I32),
+            vm((tiles, LANES), F32), vm((16, 4, 8, LANES), F32), vm((batches // 8, 25, 8, LANES), F32), vm((25, 8, LANES), F32),
+            sm((batches,), I32), sm((slots,), I32), sm((ITERS,), I32),
+            vm((1, LANES), I32), vm((PLANE, 1, LANES), I32), vm((NZ, 1, LANES), I32),
             vm((ITERS, 1, LANES), F32), vm((ITERS, PLANE, 1, LANES), F32),
             vm((ITERS, 1, LANES), F32), vm((ITERS, NZ, 1, LANES), F32),
             vm((ITERS, 16, LANES), F32), vm((ITERS, PLANE, 16, LANES), F32),
-            vm((ITERS, 32, LANES), F32), vm((ITERS, NZ, 32, LANES), F32),
-            vm((ITERS, PLANE, 16, LANES), F32), vm((ITERS, PLANE, 16, LANES), F32),
+            vm((32, LANES), F32), vm((NZ, 32, LANES), F32),
+            vm((ITERS, NZ, 16, LANES), F32), vm((ITERS, NZ, 16, LANES), F32),
             vm((32, LANES), F32), vm((NY, 32, LANES), F32),
-            vm((LANES, PLANE * 64), jnp.bfloat16), vm((96, PLANE * 64), jnp.bfloat16),
-            dma((6,)),
+            vm((NZ * 64 + LANES, PLANE * 64), jnp.bfloat16), vm((96, PLANE * 64), jnp.bfloat16),
+            dma((9,)),
             dma((31,)), dma((PLANE,)),
+            dma((7,)), dma((NZ,)),
             dma((ITERS, 31)), dma((ITERS, PLANE)),
             dma((ITERS, 7)), dma((ITERS, NZ)),
             dma((ITERS, 31)), dma((ITERS, PLANE)),
+            dma((7,)), dma((NZ,)),
             dma((ITERS, 7)), dma((ITERS, NZ)),
-            dma((ITERS, 31)), dma((ITERS, PLANE)),
             dma((3,)), dma((NY,)),
         ],
         compiler_params=pltpu.CompilerParams(collective_id=0, has_side_effects=True),

time: 81.3 us -> 67.4 us (0.83)
  the two profiles are of different devices: /device:TPU:1 before, /device:TPU:2 now
where the time goes in v2:
time: 67.4 us; the launch traced here: 67.1 us
  Pallas kernels  63.5 us (94%)
  local copies, waits for them, and re-layouts  2.95 us (4%)
    pallas_call x1, Pallas kernels, local(): pl.pallas_call(functools.partial(kernel, tiles, batches, scale), out_shap...  63.5 us
    unnamed x2, local copies, waits for them, and re-layouts  2.95 us

profile of v2, /device:TPU:2, one launch (start us, length us, event | category | flops | bytes accessed | tf_op | source)
XLA Modules:
  0.0 67.1 jit_solution(17164951887994098589)
XLA Ops:
  0.6 63.5 %shard_map.104 = (f32[128,128]{1,0:T(8,128)}, f32[25,512]{1,0:T(8,128)}) custom-call(f32[128,128]{1,0:T(8,128)} %bitcast.4, f32[128,128]{1,0:T(8,128)} %bitcast.5, f32[128,128]{1,0:T(8,128)} %bitcast.6, f32[25,16384]{1,0:T(8,128)} %basis_hbm.1, f32[8,16384]{1,0:T(8,128)} %rho_hbm.1, f32[8,16384]{1,0:T(8,128)} %res_hbm.1, s32[64]{0:T(128)} %atom_hbm.1, ...), custom_call_target="tpu_custom_call" | custom-call | tf_op jit(solution)/shard_map/pallas_call | solution.py:461
  64.2 1.5 %copy.13 = f32[16384]{0:T(1024)} copy(f32[16384]{0:T(1024)} %bitcast.7) | data formatting | bytes 131072
  65.6 1.5 %copy.14 = f32[25,512]{1,0:T(8,128)} copy(f32[25,512]{1,0:T(8,128)} %get-tuple-element.9) | data formatting | bytes 102400

commit v3 on v2

--- a/solution.py
+++ b/solution.py
@@ -78,30 +78,23 @@
     low = lane < 64
 
     def to_peers(targets, src, dst, slot, ssem, rsem, per_peer=False):
-        copies = []
-        for n, (pg, pa, pslot) in enumerate(targets):
-            copy = pltpu.make_async_remote_copy(
+        for pg, pa, pslot in targets:
+            pltpu.make_async_remote_copy(
                 src_ref=src.at[pslot] if per_peer else src,
                 dst_ref=dst.at[slot],
-                send_sem=ssem.at[n],
-                recv_sem=rsem.at[slot],
+                send_sem=ssem,
+                recv_sem=rsem,
                 device_id=(pg, pa),
                 device_id_type=MESH,
-            )
-            copy.start()
-            copies.append(copy)
-        return copies
-
-    def arrived(targets, src, dst, ssem, rsem, per_peer=False):
-        for n, (pg, pa, pslot) in enumerate(targets):
-            pltpu.make_async_remote_copy(
-                src_ref=src.at[pslot] if per_peer else src,
-                dst_ref=dst.at[pslot],
-                send_sem=ssem.at[n],
-                recv_sem=rsem.at[pslot],
-                device_id=(pg, pa),
-                device_id_type=MESH,
-            ).wait_recv()
+            ).start()
+        sends.append((dst, len(targets), ssem))
+
+    def all_bytes(dst, count, sem):
+        span = dst.at[pl.ds(0, count)]
+        pltpu.make_async_copy(span, span, sem).wait()
+
+    def arrived(targets, dst, rsem):
+        all_bytes(dst, len(targets), rsem)
 
     def tree_sum(parts):
         parts = list(parts)
@@ -136,17 +129,17 @@
 
     def all_summed(row, it):
         irow_send[it] = row[0:1]
-        sends.extend(to_peers(peers, irow_send.at[it], irow_recv.at[it], me, irow_ss.at[it], irow_rs.at[it]))
+        to_peers(peers, irow_send.at[it], irow_recv.at[it], me, irow_ss.at[it], irow_rs.at[it])
         return row
 
     def plane_sum(it):
-        arrived(peers, irow_send.at[it], irow_recv.at[it], irow_ss.at[it], irow_rs.at[it])
+        arrived(peers, irow_recv.at[it], irow_rs.at[it])
         row = tree_sum([irow_send[it]] + [irow_recv[it, pslot] for _, _, pslot in peers])
         zrow_send[it] = row
-        sends.extend(to_peers(zpeers, zrow_send.at[it], zrow_recv.at[it], z, zrow_ss.at[it], zrow_rs.at[it]))
+        to_peers(zpeers, zrow_send.at[it], zrow_recv.at[it], z, zrow_ss.at[it], zrow_rs.at[it])
 
     def slice_sum(it):
-        arrived(zpeers, zrow_send.at[it], zrow_recv.at[it], zrow_ss.at[it], zrow_rs.at[it])
+        arrived(zpeers, zrow_recv.at[it], zrow_rs.at[it])
         row = tree_sum([zrow_send[it]] + [zrow_recv[it, pslot] for _, _, pslot in zpeers])
         return jnp.broadcast_to(row, (8, LANES))
 
@@ -324,8 +317,6 @@
     accs = lax.fori_loop(0, tiles // 4, products, (jnp.zeros((8, LANES), F32),) * 5)
     first_row = row_of([jnp.sum(acc, axis=1, keepdims=True) for acc in accs])
 
-    loads[2].wait()
-    history_moments()
     for load in loads[3:6]:
         load.wait()
 
@@ -339,15 +330,17 @@
 
     pl.semaphore_wait(barrier, len(peers) + len(zpeers))
     all_summed(first_row, 0)
-    sends.extend(to_peers(peers, slot_send, slot_recv, me, slot_ss, slot_rs))
-    sends.extend(to_peers(zpeers, slot_send, zslot_recv, z, zslot_ss, zslot_rs))
+    to_peers(peers, slot_send, slot_recv, me, slot_ss, slot_rs)
+    to_peers(zpeers, slot_send, zslot_recv, z, zslot_ss, zslot_rs)
+    loads[2].wait()
+    history_moments()
     for load in loads[6:]:
         load.wait()
 
     plane_sum(0)
 
-    arrived(peers, slot_send, slot_recv, slot_ss, slot_rs)
-    arrived(zpeers, slot_send, zslot_recv, zslot_ss, zslot_rs)
+    arrived(peers, slot_recv, slot_rs)
+    arrived(zpeers, zslot_recv, zslot_rs)
     first_slot = atom * 512 + y * LANES
     sources = []
     for pair in range(PLANE // 2):
@@ -381,23 +374,21 @@
         for rows, value in zip((pl.ds(0, 8), pl.ds(8, 8)), packed(*raw_moments(coeffs, column))):
             raw_send[it, rows, :] = value
             raw_recv[it, me, rows, :] = value
-        sends.extend(to_peers(peers, raw_send.at[it], raw_recv.at[it], me, raw_ss.at[it], raw_rs.at[it]))
-        arrived(peers, raw_send.at[it], raw_recv.at[it], raw_ss.at[it], raw_rs.at[it])
+        to_peers(peers, raw_send.at[it], raw_recv.at[it], me, raw_ss.at[it], raw_rs.at[it])
+        arrived(peers, raw_recv.at[it], raw_rs.at[it])
         gather_parts(it)
         if last:
             owner_partial()
-            sends.extend(to_peers(zpeers, part_send, part_recv, z, part_ss, part_rs))
+            to_peers(zpeers, part_send, part_recv, z, part_ss, part_rs)
         peer_values(it)
-        sends.extend(
-            to_peers(zpeers, back_send.at[it], back_recv.at[it], z, back_ss.at[it], back_rs.at[it], per_peer=True)
-        )
+        to_peers(zpeers, back_send.at[it], back_recv.at[it], z, back_ss.at[it], back_rs.at[it], per_peer=True)
         if last:
-            arrived(zpeers, part_send, part_recv, part_ss, part_rs)
+            arrived(zpeers, part_recv, part_rs)
             block = tree_sum([part_send[...]] + [part_recv[pslot] for _, _, pslot in zpeers]) * scale
             blk_send[...] = block
-            sends.extend(to_peers(ypeers, blk_send, blk_recv, y, blk_ss, blk_rs))
+            to_peers(ypeers, blk_send, blk_recv, y, blk_ss, blk_rs)
             blk_recv[y] = block
-        arrived(zpeers, back_send.at[it], back_recv.at[it], back_ss.at[it], back_rs.at[it], per_peer=True)
+        arrived(zpeers, back_recv.at[it], back_rs.at[it])
         mine = tree_sum([back_send[it, z]] + [back_recv[it, pslot] for _, _, pslot in zpeers])
         at_batch = tuple(damped(kt, t) for kt, t in enumerate(unpacked(mine[0:8], mine[8:16])))
         hist_at = hist_sm[it]
@@ -427,7 +418,7 @@
                     acc = acc + r * jnp.broadcast_to(weighed[u : u + 1], (8, LANES))
             return tuple(pltpu.roll(t, LANES - 4, 1) for t in at_tiles), acc
 
-        _, acc = lax.fori_loop(0, batches // 4, density_step, (at_batch, jnp.zeros((8, LANES), F32)))
+        _, acc = lax.fori_loop(0, batches // 4, density_step, (at_batch, jnp.zeros((8, LANES), F32)), unroll=4)
         if not last:
             mine_new = jnp.broadcast_to(jnp.sum(acc, axis=1, keepdims=True), (8, LANES))
             columns = [
@@ -440,11 +431,11 @@
             row_j = (row_i - lane // 8 + 8) % 8
             total = jnp.where((row_i == hist_at) | (row_j == hist_at), slice_sum(it + 1), total)
 
-    arrived(ypeers, blk_send, blk_recv, blk_ss, blk_rs)
+    arrived(ypeers, blk_recv, blk_rs)
     for q in range(NY):
         mom_out[:, q * LANES : (q + 1) * LANES] = blk_recv[q, 0:LM]
-    for copy in sends:
-        copy.wait_send()
+    for dst, count, ssem in sends:
+        all_bytes(dst, count, ssem)
 
 
 def local(weights, target, coupling, multipole_basis, rho_hist, res_hist, batch_atom, owner_slot, slot_index):
@@ -460,7 +451,7 @@
     vmem = pl.BlockSpec(memory_space=pltpu.VMEM)
     density, moments = pl.pallas_call(
         functools.partial(kernel, tiles, batches, scale),
-        out_shape=(jax.ShapeDtypeStruct((tiles, LANES), F32), jax.ShapeDtypeStruct((LM, owned), F32)),
+        out_shape=(pltpu.VMEM((tiles, LANES), F32), pltpu.VMEM((LM, owned), F32)),
         in_specs=[anywhere] * 9,
         out_specs=(vmem, vmem),
         scratch_shapes=[
@@ -477,14 +468,8 @@
             vm((32, LANES), F32), vm((NY, 32, LANES), F32),
             vm((NZ * 64 + LANES, PLANE * 64), jnp.bfloat16), vm((96, PLANE * 64), jnp.bfloat16),
             dma((9,)),
-            dma((31,)), dma((PLANE,)),
-            dma((7,)), dma((NZ,)),
-            dma((ITERS, 31)), dma((ITERS, PLANE)),
-            dma((ITERS, 7)), dma((ITERS, NZ)),
-            dma((ITERS, 31)), dma((ITERS, PLANE)),
-            dma((7,)), dma((NZ,)),
-            dma((ITERS, 7)), dma((ITERS, NZ)),
-            dma((3,)), dma((NY,)),
+            dma, dma, dma, dma, dma((ITERS,)), dma((ITERS,)), dma((ITERS,)), dma((ITERS,)),
+            dma((ITERS,)), dma((ITERS,)), dma, dma, dma((ITERS,)), dma((ITERS,)), dma, dma,
         ],
         compiler_params=pltpu.CompilerParams(collective_id=0, has_side_effects=True),
     )(

time: 67.4 us -> 57.7 us (0.86)
  Pallas kernels: 63.5 us -> 55.6 us
  local copies, waits for them, and re-layouts: 2.95 us -> 1.26 us
    pallas_call x1, Pallas kernels: 63.5 us -> 55.6 us  [local(): pl.pallas_call(functools.partial(kernel, tiles, batches, scale), out_shap...]
    unnamed x2, local copies, waits for them, and re-layouts: 2.95 us -> 1.26 us
where the time goes in v3:
time: 57.7 us; the launch traced here: 57.5 us
  Pallas kernels  55.6 us (96%)
  local copies, waits for them, and re-layouts  1.26 us (2%)
  between operations  0.64 us (1%)
    pallas_call x1, Pallas kernels, local(): pl.pallas_call(functools.partial(kernel, tiles, batches, scale), out_shap...  55.6 us
    unnamed x2, local copies, waits for them, and re-layouts  1.26 us

profile of v3, /device:TPU:2, one launch (start us, length us, event | category | flops | bytes accessed | tf_op | source)
XLA Modules:
  0.0 57.5 jit_solution(2050487810322883255)
XLA Ops:
  0.6 55.6 %shard_map.104 = (f32[128,128]{1,0:T(8,128)S(1)}, f32[25,512]{1,0:T(8,128)S(1)}) custom-call(f32[128,128]{1,0:T(8,128)} %bitcast.5, f32[128,128]{1,0:T(8,128)} %bitcast.6, f32[128,128]{1,0:T(8,128)} %bitcast.7, f32[25,16384]{1,0:T(8,128)} %basis_hbm.1, f32[8,16384]{1,0:T(8,128)} %rho_hbm.1, f32[8,16384]{1,0:T(8,128)} %res_hbm.1, s32[64]{0:T(128)} %atom_hbm.1, ...), custom_call_target="tpu_custom_call" | custom-call | tf_op jit(solution)/shard_map/pallas_call | solution.py:452
  56.3 0.6 %copy.13 = f32[16384]{0:T(1024)} copy(f32[16384]{0:T(1024)S(1)} %bitcast.4) | data formatting | bytes 131072
  56.9 0.6 %copy.14 = f32[25,512]{1,0:T(8,128)} copy(f32[25,512]{1,0:T(8,128)S(1)} %get-tuple-element.7) | data formatting | bytes 102400

commit v4 on v3

--- a/solution.py
+++ b/solution.py
@@ -30,10 +30,10 @@
     atom_sm, owner_sm, hist_sm,
     slot_send, slot_recv, zslot_recv, irow_send, irow_recv, zrow_send, zrow_recv,
     raw_send, raw_recv, part_send, part_recv, back_send, back_recv, blk_send, blk_recv,
-    match, xparts,
+    keep_send, kept, match, xparts,
     load_sem,
     slot_ss, slot_rs, zslot_ss, zslot_rs, irow_ss, irow_rs, zrow_ss, zrow_rs,
-    raw_ss, raw_rs, part_ss, part_rs, back_ss, back_rs, blk_ss, blk_rs,
+    raw_ss, raw_rs, part_ss, part_rs, back_ss, back_rs, blk_ss, blk_rs, keep_ss, keep_rs, pair_ss, pair_rs,
 ):
     grid = lax.axis_index("grid")
     atom = lax.axis_index("atom")
@@ -55,6 +55,9 @@
     for dz in (4, 3, 5, 2, 6, 1, 7):
         pz = (z + dz) % NZ
         zpeers.append((pz * NY + y, atom, pz))
+    spot = y * NX + x
+    alike = [(pg, xs[dx] * NC + c, 0) for dy in (2, 1, 3, 0) for dx in (2, 1, 3, 0) if dy or dx for pg in [z * NY + ys[dy]]]
+    other = [(grid, x * NC + cs[1], 0)]
     ypeers = [(z * NY + ys[dy], atom, ys[dy]) for dy in (2, 1, 3)]
 
     barrier = pltpu.get_barrier_semaphore()
@@ -222,7 +225,7 @@
         for n in range(25):
             hist_moms[n] = joined(n)
 
-    def fresh_moments(hist_at):
+    def fresh_moments():
         def step(group, carry):
             weigh(group)
             for kt in range(4):
@@ -230,11 +233,7 @@
             return carry
 
         lax.fori_loop(0, batches // 8, step, 0)
-        for kt in range(3):
-            value = joined(kt)
-            for i in range(H):
-                hist_moms[i * 3 + kt] = jnp.where(hist_at == i, value, hist_moms[i * 3 + kt])
-        hist_moms[24] = jnp.where(sub == hist_at, joined(3), hist_moms[24])
+        return [joined(kt) for kt in range(4)]
 
     def raw_moments(coeffs, column):
         return [tree_sum([coeffs[i] * hist_moms[i * 3 + kt] for i in range(H)]) for kt in range(3)] + [
@@ -264,12 +263,47 @@
     def pair_joined(a, b):
         return jnp.where(low, a, pltpu.roll(b, 64, 1)), jnp.where(low, pltpu.roll(a, 64, 1), b)
 
-    def gather_parts(it):
+    def keep_moments(hist_at):
+        def stays(j, kt):
+            return jnp.where(hist_at > j, hist_moms[j * 3 + kt], hist_moms[(j + 1) * 3 + kt])
+
+        tiles_of = [jnp.where(low, stays(j, 0), stays(j, 1)) for j in range(7)]
+        tiles_of += [jnp.where(low, stays(2 * m, 2), stays(2 * m + 1, 2)) for m in range(3)]
+        tiles_of += [jnp.where(low, stays(6, 2), hist_moms[24])]
+        for n, value in enumerate(tiles_of):
+            keep_send[n * 8 : n * 8 + 8, :] = value
+            kept[c, spot, n * 8 : n * 8 + 8, :] = value
+
+    def combined(coeffs, column, hist_at):
+        own = [jnp.where(hist_at > j, coeffs[j], coeffs[j + 1]) for j in range(7)]
+        fresh_share = tree_sum([jnp.where(hist_at == i, coeffs[i], 0.0) for i in range(H)])
+        doubles = [jnp.where(low, own[2 * m], own[2 * m + 1]) for m in range(3)]
+        tail = jnp.where(low, own[6], jnp.where(sub == hist_at, 0.0, column))
+
+        def of(core, at, new_first, new_second):
+            t = [kept[core, at, n * 8 : n * 8 + 8, :] for n in range(11)]
+            first = tree_sum([own[j] * t[j] for j in range(7)] + [fresh_share * new_first])
+            u = tree_sum([doubles[m] * t[7 + m] for m in range(3)])
+            v = tail * t[10]
+            turned = pltpu.roll(v, 64, 1)
+            t2 = u + pltpu.roll(u, 64, 1) + jnp.where(low, v, turned)
+            second = jnp.where(
+                sub < 4,
+                jnp.where(low, t2, pltpu.roll(t2, 4, 0)),
+                jnp.where((sub == 4) & low, over_subs(turned), 0.0),
+            )
+            return first, second + fresh_share * new_second
+
+        return of
+
+    def gather_parts(it, combine=None):
         for pair in range(PLANE // 2):
             cols = pl.ds(pair * LANES, LANES)
+            raws = [[raw_recv[it, 2 * pair + core, pl.ds(half * 8, 8), :] for half in range(2)] for core in range(2)]
+            if combine:
+                raws = [combine(core, pair, *raws[core]) for core in range(2)]
             for half in range(2):
-                rows = pl.ds(half * 8, 8)
-                a, b = pair_joined(raw_recv[it, 2 * pair, rows, :], raw_recv[it, 2 * pair + 1, rows, :])
+                a, b = pair_joined(raws[0][half], raws[1][half])
                 both = jnp.concatenate([a, b], axis=0)
                 for n, part in enumerate(three(both)):
                     xparts[pl.ds(n * 32 + half * 16, 16), cols] = part
@@ -299,6 +333,12 @@
         k = sub + kt * 8
         damp = jnp.where(k < 1, 1.0, jnp.where(k < 4, 1 / 2, jnp.where(k < 9, 1 / 3, jnp.where(k < 16, 1 / 4, 1 / 5))))
         return value * (damp * (scale * BETA))
+
+    def send_raw(it, values):
+        for rows, value in zip((pl.ds(0, 8), pl.ds(8, 8)), packed(*values)):
+            raw_send[it, rows, :] = value
+            raw_recv[it, me, rows, :] = value
+        to_peers(peers, raw_send.at[it], raw_recv.at[it], me, raw_ss.at[it], raw_rs.at[it])
 
     loads[0].wait()
     loads[1].wait()
@@ -317,6 +357,8 @@
     accs = lax.fori_loop(0, tiles // 4, products, (jnp.zeros((8, LANES), F32),) * 5)
     first_row = row_of([jnp.sum(acc, axis=1, keepdims=True) for acc in accs])
 
+    pl.semaphore_wait(barrier, len(peers) + len(zpeers))
+    all_summed(first_row, 0)
     for load in loads[3:6]:
         load.wait()
 
@@ -327,9 +369,6 @@
     slot_send[...] = slots[0:1]
     slot_recv[me] = slots[0:1]
     zslot_recv[z] = slots[0:1]
-
-    pl.semaphore_wait(barrier, len(peers) + len(zpeers))
-    all_summed(first_row, 0)
     to_peers(peers, slot_send, slot_recv, me, slot_ss, slot_rs)
     to_peers(zpeers, slot_send, zslot_recv, z, zslot_ss, zslot_rs)
     loads[2].wait()
@@ -371,12 +410,14 @@
     for it in range(ITERS):
         last = it == ITERS - 1
         coeffs, column = mixing(total)
-        for rows, value in zip((pl.ds(0, 8), pl.ds(8, 8)), packed(*raw_moments(coeffs, column))):
-            raw_send[it, rows, :] = value
-            raw_recv[it, me, rows, :] = value
-        to_peers(peers, raw_send.at[it], raw_recv.at[it], me, raw_ss.at[it], raw_rs.at[it])
-        arrived(peers, raw_recv.at[it], raw_rs.at[it])
-        gather_parts(it)
+        if last:
+            gather_parts(it, combined(coeffs, column, hist_sm[0]))
+        else:
+            send_raw(it, raw_moments(coeffs, column))
+            keep_moments(hist_sm[it])
+            arrived(peers, raw_recv.at[it], raw_rs.at[it])
+            to_peers(alike, keep_send, kept.at[c], spot, keep_ss, keep_rs)
+            gather_parts(it)
         if last:
             owner_partial()
             to_peers(zpeers, part_send, part_recv, z, part_ss, part_rs)
@@ -425,8 +466,12 @@
                 jnp.where(sub == hist_at, pltpu.roll(mine_new, d, 0) if d else mine_new, mine_new) for d in range(5)
             ]
             all_summed(row_of(columns), it + 1)
-            fresh_moments(hist_at)
+            send_raw(it + 1, fresh_moments())
+            arrived(alike, kept.at[0], keep_rs)
+            to_peers(other, kept.at[c], kept, c, pair_ss, pair_rs)
             plane_sum(it + 1)
+            arrived(peers, raw_recv.at[it + 1], raw_rs.at[it + 1])
+            arrived(other, kept, pair_rs)
             row_i = lane % 8
             row_j = (row_i - lane // 8 + 8) % 8
             total = jnp.where((row_i == hist_at) | (row_j == hist_at), slice_sum(it + 1), total)
@@ -466,10 +511,11 @@
             vm((32, LANES), F32), vm((NZ, 32, LANES), F32),
             vm((ITERS, NZ, 16, LANES), F32), vm((ITERS, NZ, 16, LANES), F32),
             vm((32, LANES), F32), vm((NY, 32, LANES), F32),
+            vm((88, LANES), F32), vm((NC, NY * NX, 88, LANES), F32),
             vm((NZ * 64 + LANES, PLANE * 64), jnp.bfloat16), vm((96, PLANE * 64), jnp.bfloat16),
             dma((9,)),
             dma, dma, dma, dma, dma((ITERS,)), dma((ITERS,)), dma((ITERS,)), dma((ITERS,)),
-            dma((ITERS,)), dma((ITERS,)), dma, dma, dma((ITERS,)), dma((ITERS,)), dma, dma,
+            dma((ITERS,)), dma((ITERS,)), dma, dma, dma((ITERS,)), dma((ITERS,)), dma, dma, dma, dma, dma, dma,
         ],
         compiler_params=pltpu.CompilerParams(collective_id=0, has_side_effects=True),
     )(

time: 57.7 us -> 52 us (0.901)
  Pallas kernels: 55.6 us -> 50 us
    pallas_call x1, Pallas kernels: 55.6 us -> 50 us  [local(): pl.pallas_call(functools.partial(kernel, tiles, batches, scale), out_shap...]
where the time goes in v4:
time: 52 us; the launch traced here: 51.9 us
  Pallas kernels  50 us (96%)
  local copies, waits for them, and re-layouts  1.26 us (2%)
  between operations  0.64 us (1%)
    pallas_call x1, Pallas kernels, local(): pl.pallas_call(functools.partial(kernel, tiles, batches, scale), out_shap...  50 us
    unnamed x2, local copies, waits for them, and re-layouts  1.26 us

profile of v4, /device:TPU:2, one launch (start us, length us, event | category | flops | bytes accessed | tf_op | source)
XLA Modules:
  0.0 51.9 jit_solution(13875028629859761020)
XLA Ops:
  0.6 50.0 %shard_map.104 = (f32[128,128]{1,0:T(8,128)S(1)}, f32[25,512]{1,0:T(8,128)S(1)}) custom-call(f32[128,128]{1,0:T(8,128)} %bitcast.5, f32[128,128]{1,0:T(8,128)} %bitcast.6, f32[128,128]{1,0:T(8,128)} %bitcast.7, f32[25,16384]{1,0:T(8,128)} %basis_hbm.1, f32[8,16384]{1,0:T(8,128)} %rho_hbm.1, f32[8,16384]{1,0:T(8,128)} %res_hbm.1, s32[64]{0:T(128)} %atom_hbm.1, ...), custom_call_target="tpu_custom_call" | custom-call | tf_op jit(solution)/shard_map/pallas_call | solution.py:497
  50.7 0.6 %copy.13 = f32[16384]{0:T(1024)} copy(f32[16384]{0:T(1024)S(1)} %bitcast.4) | data formatting | bytes 131072
  51.3 0.6 %copy.14 = f32[25,512]{1,0:T(8,128)} copy(f32[25,512]{1,0:T(8,128)S(1)} %get-tuple-element.7) | data formatting | bytes 102400

commit v5 on v4

--- a/solution.py
+++ b/solution.py
@@ -30,7 +30,7 @@
     atom_sm, owner_sm, hist_sm,
     slot_send, slot_recv, zslot_recv, irow_send, irow_recv, zrow_send, zrow_recv,
     raw_send, raw_recv, part_send, part_recv, back_send, back_recv, blk_send, blk_recv,
-    keep_send, kept, match, xparts,
+    keep_send, kept, match, xparts, xkept, own_kept, own_fresh,
     load_sem,
     slot_ss, slot_rs, zslot_ss, zslot_rs, irow_ss, irow_rs, zrow_ss, zrow_rs,
     raw_ss, raw_rs, part_ss, part_rs, back_ss, back_rs, blk_ss, blk_rs, keep_ss, keep_rs, pair_ss, pair_rs,
@@ -52,8 +52,8 @@
                     pa = xs[dx] * NC + cs[dc]
                     peers.append((z * NY + ys[dy], pa, ys[dy] * (NX * NC) + pa))
     zpeers = []
-    for dz in (4, 3, 5, 2, 6, 1, 7):
-        pz = (z + dz) % NZ
+    zorder = [(z + dz) % NZ for dz in (4, 3, 5, 2, 6, 1, 7, 0)]
+    for pz in zorder[:-1]:
         zpeers.append((pz * NY + y, atom, pz))
     spot = y * NX + x
     alike = [(pg, xs[dx] * NC + c, 0) for dy in (2, 1, 3, 0) for dx in (2, 1, 3, 0) if dy or dx for pg in [z * NY + ys[dy]]]
@@ -80,17 +80,18 @@
     lane = lax.broadcasted_iota(I32, (8, LANES), 1)
     low = lane < 64
 
-    def to_peers(targets, src, dst, slot, ssem, rsem, per_peer=False):
+    def to_peers(targets, src, dst, slot, ssem, rsem, later=False):
         for pg, pa, pslot in targets:
             pltpu.make_async_remote_copy(
-                src_ref=src.at[pslot] if per_peer else src,
+                src_ref=src,
                 dst_ref=dst.at[slot],
                 send_sem=ssem,
                 recv_sem=rsem,
                 device_id=(pg, pa),
                 device_id_type=MESH,
             ).start()
-        sends.append((dst, len(targets), ssem))
+        if not later:
+            sends.append((dst, len(targets), ssem))
 
     def all_bytes(dst, count, sem):
         span = dst.at[pl.ds(0, count)]
@@ -253,6 +254,9 @@
         t3 = jnp.where(sub == 0, pltpu.roll(second, 4, 0), 0.0)
         return first, pltpu.roll(first, 64, 1), t2, t3
 
+    def both_tiles(load):
+        return load(pl.ds(0, 8)), pltpu.roll(load(pl.ds(5, 8)), 5, 0)
+
     def three(v):
         hi = v.astype(jnp.bfloat16)
         rest = v - hi.astype(F32)
@@ -274,11 +278,14 @@
             keep_send[n * 8 : n * 8 + 8, :] = value
             kept[c, spot, n * 8 : n * 8 + 8, :] = value
 
-    def combined(coeffs, column, hist_at):
+    def shares(coeffs, column, hist_at):
         own = [jnp.where(hist_at > j, coeffs[j], coeffs[j + 1]) for j in range(7)]
         fresh_share = tree_sum([jnp.where(hist_at == i, coeffs[i], 0.0) for i in range(H)])
+        return own, fresh_share, jnp.where(sub == hist_at, 0.0, column)
+
+    def combined(own, fresh_share, stay_column):
         doubles = [jnp.where(low, own[2 * m], own[2 * m + 1]) for m in range(3)]
-        tail = jnp.where(low, own[6], jnp.where(sub == hist_at, 0.0, column))
+        tail = jnp.where(low, own[6], stay_column)
 
         def of(core, at, new_first, new_second):
             t = [kept[core, at, n * 8 : n * 8 + 8, :] for n in range(11)]
@@ -299,7 +306,7 @@
     def gather_parts(it, combine=None):
         for pair in range(PLANE // 2):
             cols = pl.ds(pair * LANES, LANES)
-            raws = [[raw_recv[it, 2 * pair + core, pl.ds(half * 8, 8), :] for half in range(2)] for core in range(2)]
+            raws = [both_tiles(lambda rows: raw_recv[it, 2 * pair + core, rows, :]) for core in range(2)]
             if combine:
                 raws = [combine(core, pair, *raws[core]) for core in range(2)]
             for half in range(2):
@@ -314,20 +321,43 @@
         )
         return sums[0:32] + sums[32:64] + sums[64:96]
 
-    def owner_partial():
-        sums = matched(NZ * 64, LANES)
-        part_send[0:16] = sums[0:16]
-        part_send[16:24] = jnp.where(sub < 4, sums[16:24], pltpu.roll(sums[24:32], 4, 0))
-        part_send[24:32] = jnp.where(sub < 1, pltpu.roll(sums[16:24], 4, 0), 0.0)
-
-    def peer_values(it):
-        picked = matched(0, NZ * 64)
-        for pair in range(NZ // 2):
+    def owner_kept():
+        for pair in range(PLANE // 2):
+            cols = pl.ds(pair * LANES, LANES)
+            for n in range(11):
+                both = pair_joined(kept[0, pair, n * 8 : n * 8 + 8, :], kept[1, pair, n * 8 : n * 8 + 8, :])
+                for m, part in enumerate(three(jnp.concatenate(both, axis=0))):
+                    xkept[pl.ds(m * 176 + n * 16, 16), cols] = part
+        sums = lax.dot_general(
+            xkept[...], match[pl.ds(NZ * 64, LANES), :], (((1,), (1,)), ((), ())), preferred_element_type=F32
+        )
+        own_kept[...] = sums[0:176] + sums[176:352] + sums[352:528]
+
+    def owner_fresh(it):
+        gather_parts(it)
+        own_fresh[...] = matched(NZ * 64, LANES)
+
+    def owner_partial(own, fresh_share, stay_column):
+        def of(n):
+            return own_kept[n * 8 : n * 8 + 8]
+
+        new = [fresh_share * own_fresh[n * 8 : n * 8 + 8] for n in range(4)]
+        part_send[0:8] = tree_sum([own[j] * of(2 * j) for j in range(7)] + [new[0]])
+        part_send[8:16] = tree_sum([own[j] * of(2 * j + 1) for j in range(7)] + [new[1]])
+        part_send[16:24] = tree_sum(
+            [own[j] * of(14 + j) for j in range(7)] + [jnp.where(sub < 4, new[2], pltpu.roll(new[3], 4, 0))]
+        )
+        part_send[24:25] = (over_subs(stay_column * of(21)) + pltpu.roll(new[2], 4, 0))[0:1]
+
+    def peer_values(it, first):
+        picked = matched(first * 64, 256)
+        for pair in range(2):
             cols = slice(pair * LANES, (pair + 1) * LANES)
             for half in range(2):
-                a, b = pair_joined(picked[half * 16 : half * 16 + 8, cols], picked[half * 16 + 8 : half * 16 + 16, cols])
-                back_send[it, 2 * pair, half * 8 : half * 8 + 8, :] = a
-                back_send[it, 2 * pair + 1, half * 8 : half * 8 + 8, :] = b
+                values = pair_joined(picked[half * 16 : half * 16 + 8, cols], picked[half * 16 + 8 : half * 16 + 16, cols])
+                for n, value in enumerate(values):
+                    size = 5 if half else 8
+                    back_send[it, first + 2 * pair + n, half * 8 : half * 8 + size, :] = value[0:size]
 
     def damped(kt, value):
         k = sub + kt * 8
@@ -335,9 +365,10 @@
         return value * (damp * (scale * BETA))
 
     def send_raw(it, values):
-        for rows, value in zip((pl.ds(0, 8), pl.ds(8, 8)), packed(*values)):
-            raw_send[it, rows, :] = value
-            raw_recv[it, me, rows, :] = value
+        first, second = packed(*values)
+        for ref, at in ((raw_send, (it,)), (raw_recv, (it, me))):
+            ref[(*at, pl.ds(0, 8))] = first
+            ref[(*at, pl.ds(8, 5))] = second[0:5]
         to_peers(peers, raw_send.at[it], raw_recv.at[it], me, raw_ss.at[it], raw_rs.at[it])
 
     loads[0].wait()
@@ -392,17 +423,19 @@
             halves = [jnp.where(sources[pair] == one, 1.0, 0.0) for one in wanted]
             match[pl.ds(at, 16), pl.ds(pair * LANES, LANES)] = jnp.concatenate(halves, axis=0).astype(jnp.bfloat16)
 
-    def target_step(step_at, carry):
-        row = jnp.broadcast_to(zslot_recv[step_at // 4], (8, LANES)).astype(F32)
-        wanted = []
-        for h in range(2):
-            hit = lane == sub + ((step_at % 4) * 16 + h * 8)
-            column = jnp.sum(jnp.where(hit, row, 0.0), axis=1, keepdims=True)
-            wanted.append(jnp.broadcast_to(column, (8, LANES)).astype(I32))
-        match_rows(pl.multiple_of(step_at * 16, 16), wanted)
-        return carry
-
-    lax.fori_loop(0, NZ * 4, target_step, 0)
+    for block, pz in enumerate(zorder):
+        row = jnp.broadcast_to(zslot_recv[pz], (8, LANES)).astype(F32)
+
+        def target_step(st, carry):
+            wanted = []
+            for h in range(2):
+                hit = lane == sub + (st * 16 + h * 8)
+                column = jnp.sum(jnp.where(hit, row, 0.0), axis=1, keepdims=True)
+                wanted.append(jnp.broadcast_to(column, (8, LANES)).astype(I32))
+            match_rows(pl.multiple_of(block * 64 + st * 16, 16), wanted)
+            return carry
+
+        lax.fori_loop(0, 4, target_step, 0)
     for st in range(LANES // 16):
         match_rows(NZ * 64 + st * 16, [sub + (first_slot + st * 16 + h * 8) for h in range(2)])
 
@@ -411,18 +444,21 @@
         last = it == ITERS - 1
         coeffs, column = mixing(total)
         if last:
-            gather_parts(it, combined(coeffs, column, hist_sm[0]))
+            split = shares(coeffs, column, hist_sm[0])
+            owner_partial(*split)
+            to_peers(zpeers, part_send, part_recv, z, part_ss, part_rs)
+            gather_parts(it, combined(*split))
         else:
             send_raw(it, raw_moments(coeffs, column))
             keep_moments(hist_sm[it])
             arrived(peers, raw_recv.at[it], raw_rs.at[it])
             to_peers(alike, keep_send, kept.at[c], spot, keep_ss, keep_rs)
             gather_parts(it)
-        if last:
-            owner_partial()
-            to_peers(zpeers, part_send, part_recv, z, part_ss, part_rs)
-        peer_values(it)
-        to_peers(zpeers, back_send.at[it], back_recv.at[it], z, back_ss.at[it], back_rs.at[it], per_peer=True)
+        for first in (0, 4):
+            peer_values(it, first)
+            for n, target in list(enumerate(zpeers))[first : first + 4]:
+                to_peers([target], back_send.at[it, n], back_recv.at[it], z, back_ss.at[it], back_rs.at[it], True)
+        sends.append((back_recv.at[it], len(zpeers), back_ss.at[it]))
         if last:
             arrived(zpeers, part_recv, part_rs)
             block = tree_sum([part_send[...]] + [part_recv[pslot] for _, _, pslot in zpeers]) * scale
@@ -430,8 +466,10 @@
             to_peers(ypeers, blk_send, blk_recv, y, blk_ss, blk_rs)
             blk_recv[y] = block
         arrived(zpeers, back_recv.at[it], back_rs.at[it])
-        mine = tree_sum([back_send[it, z]] + [back_recv[it, pslot] for _, _, pslot in zpeers])
-        at_batch = tuple(damped(kt, t) for kt, t in enumerate(unpacked(mine[0:8], mine[8:16])))
+        mine = both_tiles(
+            lambda rows: tree_sum([back_send[it, NZ - 1, rows, :]] + [back_recv[it, pslot, rows, :] for _, _, pslot in zpeers])
+        )
+        at_batch = tuple(damped(kt, t) for kt, t in enumerate(unpacked(*mine)))
         hist_at = hist_sm[it]
 
         def density_step(group, carry):
@@ -470,15 +508,17 @@
             arrived(alike, kept.at[0], keep_rs)
             to_peers(other, kept.at[c], kept, c, pair_ss, pair_rs)
             plane_sum(it + 1)
+            arrived(other, kept, pair_rs)
+            owner_kept()
             arrived(peers, raw_recv.at[it + 1], raw_rs.at[it + 1])
-            arrived(other, kept, pair_rs)
+            owner_fresh(it + 1)
             row_i = lane % 8
             row_j = (row_i - lane // 8 + 8) % 8
             total = jnp.where((row_i == hist_at) | (row_j == hist_at), slice_sum(it + 1), total)
 
     arrived(ypeers, blk_recv, blk_rs)
     for q in range(NY):
-        mom_out[:, q * LANES : (q + 1) * LANES] = blk_recv[q, 0:LM]
+        mom_out[:, q * LANES : (q + 1) * LANES] = blk_recv[q]
     for dst, count, ssem in sends:
         all_bytes(dst, count, ssem)
 
@@ -507,12 +547,13 @@
             vm((1, LANES), I32), vm((PLANE, 1, LANES), I32), vm((NZ, 1, LANES), I32),
             vm((ITERS, 1, LANES), F32), vm((ITERS, PLANE, 1, LANES), F32),
             vm((ITERS, 1, LANES), F32), vm((ITERS, NZ, 1, LANES), F32),
-            vm((ITERS, 16, LANES), F32), vm((ITERS, PLANE, 16, LANES), F32),
-            vm((32, LANES), F32), vm((NZ, 32, LANES), F32),
-            vm((ITERS, NZ, 16, LANES), F32), vm((ITERS, NZ, 16, LANES), F32),
-            vm((32, LANES), F32), vm((NY, 32, LANES), F32),
+            vm((ITERS, 13, LANES), F32), vm((ITERS, PLANE, 13, LANES), F32),
+            vm((LM, LANES), F32), vm((NZ, LM, LANES), F32),
+            vm((ITERS, NZ, 13, LANES), F32), vm((ITERS, NZ, 13, LANES), F32),
+            vm((LM, LANES), F32), vm((NY, LM, LANES), F32),
             vm((88, LANES), F32), vm((NC, NY * NX, 88, LANES), F32),
             vm((NZ * 64 + LANES, PLANE * 64), jnp.bfloat16), vm((96, PLANE * 64), jnp.bfloat16),
+            vm((528, PLANE * 64), jnp.bfloat16), vm((176, LANES), F32), vm((32, LANES), F32),
             dma((9,)),
             dma, dma, dma, dma, dma((ITERS,)), dma((ITERS,)), dma((ITERS,)), dma((ITERS,)),
             dma((ITERS,)), dma((ITERS,)), dma, dma, dma((ITERS,)), dma((ITERS,)), dma, dma, dma, dma, dma, dma,

time: 52 us -> 50.7 us (0.975)
  Pallas kernels: 50 us -> 48.7 us
    pallas_call x1, Pallas kernels: 50 us -> 48.7 us  [local(): pl.pallas_call(functools.partial(kernel, tiles, batches, scale), out_shap...]
where the time goes in v5:
time: 50.7 us; the launch traced here: 50.6 us
  Pallas kernels  48.7 us (96%)
  local copies, waits for them, and re-layouts  1.26 us (2%)
  between operations  0.64 us (1%)
    pallas_call x1, Pallas kernels, local(): pl.pallas_call(functools.partial(kernel, tiles, batches, scale), out_shap...  48.7 us
    unnamed x2, local copies, waits for them, and re-layouts  1.26 us

profile of v5, /device:TPU:2, one launch (start us, length us, event | category | flops | bytes accessed | tf_op | source)
XLA Modules:
  0.0 50.6 jit_solution(18054826100596042817)
XLA Ops:
  0.6 48.7 %shard_map.104 = (f32[128,128]{1,0:T(8,128)S(1)}, f32[25,512]{1,0:T(8,128)S(1)}) custom-call(f32[128,128]{1,0:T(8,128)} %bitcast.5, f32[128,128]{1,0:T(8,128)} %bitcast.6, f32[128,128]{1,0:T(8,128)} %bitcast.7, f32[25,16384]{1,0:T(8,128)} %basis_hbm.1, f32[8,16384]{1,0:T(8,128)} %rho_hbm.1, f32[8,16384]{1,0:T(8,128)} %res_hbm.1, s32[64]{0:T(128)} %atom_hbm.1, ...), custom_call_target="tpu_custom_call" | custom-call | tf_op jit(solution)/shard_map/pallas_call | solution.py:537
  49.3 0.6 %copy.13 = f32[16384]{0:T(1024)} copy(f32[16384]{0:T(1024)S(1)} %bitcast.4) | data formatting | bytes 131072
  49.9 0.6 %copy.14 = f32[25,512]{1,0:T(8,128)} copy(f32[25,512]{1,0:T(8,128)S(1)} %get-tuple-element.7) | data formatting | bytes 102400

commit v6 on v5

--- a/solution.py
+++ b/solution.py
@@ -26,14 +26,15 @@
     tiles, batches, scale,
     w_hbm, tgt_hbm, cpl_hbm, basis_hbm, rho_hbm, res_hbm, atom_hbm, owner_hbm, hist_hbm,
     dens_out, mom_out,
-    w, tgt, cpl, basis, rho, res, fresh, weighted, merged, hist_moms,
+    w, tgt, cpl, basis, rho, res, fresh, mixed, weighted, merged, hist_moms,
     atom_sm, owner_sm, hist_sm,
     slot_send, slot_recv, zslot_recv, irow_send, irow_recv, zrow_send, zrow_recv,
     raw_send, raw_recv, part_send, part_recv, back_send, back_recv, blk_send, blk_recv,
-    keep_send, kept, match, xparts, xkept, own_kept, own_fresh,
+    early_send, early, keep_send, kept, match, xparts, xkept, own_kept, own_fresh,
     load_sem,
     slot_ss, slot_rs, zslot_ss, zslot_rs, irow_ss, irow_rs, zrow_ss, zrow_rs,
     raw_ss, raw_rs, part_ss, part_rs, back_ss, back_rs, blk_ss, blk_rs, keep_ss, keep_rs, pair_ss, pair_rs,
+    early_ss, early_rs, epair_ss, epair_rs,
 ):
     grid = lax.axis_index("grid")
     atom = lax.axis_index("atom")
@@ -111,14 +112,17 @@
         v = v + pltpu.roll(v, 2, 0)
         return v + pltpu.roll(v, 1, 0)
 
+    def columns_of(at):
+        return pl.ds(at * LANES if isinstance(at, int) else pl.multiple_of(at * LANES, LANES), LANES)
+
     def tile_at(ref, at):
-        return ref[:, pl.ds(pl.multiple_of(at * LANES, LANES), LANES)]
+        return ref[:, columns_of(at)]
 
     def row_at(ref, at):
         return jnp.broadcast_to(ref[pl.ds(at, 1), :], (8, LANES))
 
     def basis_tile(kt, at):
-        cols = pl.ds(pl.multiple_of(at * LANES, LANES), LANES)
+        cols = columns_of(at)
         if kt < 3:
             return basis[pl.ds(kt * 8, 8), cols]
         return jnp.broadcast_to(basis[pl.ds(24, 1), cols], (8, LANES))
@@ -275,8 +279,13 @@
         tiles_of += [jnp.where(low, stays(2 * m, 2), stays(2 * m + 1, 2)) for m in range(3)]
         tiles_of += [jnp.where(low, stays(6, 2), hist_moms[24])]
         for n, value in enumerate(tiles_of):
-            keep_send[n * 8 : n * 8 + 8, :] = value
-            kept[c, spot, n * 8 : n * 8 + 8, :] = value
+            send, ref, at = (early_send, early, n) if n < 5 else (keep_send, kept, n - 5)
+            send[at * 8 : at * 8 + 8, :] = value
+            ref[c, spot, at * 8 : at * 8 + 8, :] = value
+
+    def kept_tile(core, at, n):
+        ref, n = (early, n) if n < 5 else (kept, n - 5)
+        return ref[core, at, n * 8 : n * 8 + 8, :]
 
     def shares(coeffs, column, hist_at):
         own = [jnp.where(hist_at > j, coeffs[j], coeffs[j + 1]) for j in range(7)]
@@ -288,7 +297,7 @@
         tail = jnp.where(low, own[6], stay_column)
 
         def of(core, at, new_first, new_second):
-            t = [kept[core, at, n * 8 : n * 8 + 8, :] for n in range(11)]
+            t = [kept_tile(core, at, n) for n in range(11)]
             first = tree_sum([own[j] * t[j] for j in range(7)] + [fresh_share * new_first])
             u = tree_sum([doubles[m] * t[7 + m] for m in range(3)])
             v = tail * t[10]
@@ -321,17 +330,18 @@
         )
         return sums[0:32] + sums[32:64] + sums[64:96]
 
-    def owner_kept():
+    def owner_kept(first, count):
+        size = count * 16
         for pair in range(PLANE // 2):
             cols = pl.ds(pair * LANES, LANES)
-            for n in range(11):
-                both = pair_joined(kept[0, pair, n * 8 : n * 8 + 8, :], kept[1, pair, n * 8 : n * 8 + 8, :])
+            for n in range(count):
+                both = pair_joined(kept_tile(0, pair, first + n), kept_tile(1, pair, first + n))
                 for m, part in enumerate(three(jnp.concatenate(both, axis=0))):
-                    xkept[pl.ds(m * 176 + n * 16, 16), cols] = part
+                    xkept[pl.ds(m * size + n * 16, 16), cols] = part
         sums = lax.dot_general(
-            xkept[...], match[pl.ds(NZ * 64, LANES), :], (((1,), (1,)), ((), ())), preferred_element_type=F32
+            xkept[pl.ds(0, 3 * size), :], match[pl.ds(NZ * 64, LANES), :], (((1,), (1,)), ((), ())), preferred_element_type=F32
         )
-        own_kept[...] = sums[0:176] + sums[176:352] + sums[352:528]
+        own_kept[first * 16 : first * 16 + size] = sums[0:size] + sums[size : 2 * size] + sums[2 * size : 3 * size]
 
     def owner_fresh(it):
         gather_parts(it)
@@ -350,8 +360,8 @@
         part_send[24:25] = (over_subs(stay_column * of(21)) + pltpu.roll(new[2], 4, 0))[0:1]
 
     def peer_values(it, first):
-        picked = matched(first * 64, 256)
-        for pair in range(2):
+        picked = matched(first * 64, LANES)
+        for pair in range(1):
             cols = slice(pair * LANES, (pair + 1) * LANES)
             for half in range(2):
                 values = pair_joined(picked[half * 16 : half * 16 + 8, cols], picked[half * 16 + 8 : half * 16 + 16, cols])
@@ -408,6 +418,8 @@
         load.wait()
 
     plane_sum(0)
+    keep_moments(hist_sm[0])
+    to_peers(alike, early_send, early.at[c], spot, early_ss, early_rs)
 
     arrived(peers, slot_recv, slot_rs)
     arrived(zpeers, zslot_recv, zslot_rs)
@@ -450,13 +462,14 @@
             gather_parts(it, combined(*split))
         else:
             send_raw(it, raw_moments(coeffs, column))
-            keep_moments(hist_sm[it])
             arrived(peers, raw_recv.at[it], raw_rs.at[it])
             to_peers(alike, keep_send, kept.at[c], spot, keep_ss, keep_rs)
+            arrived(alike, early.at[0], early_rs)
+            to_peers(other, early.at[c], early, c, epair_ss, epair_rs)
             gather_parts(it)
-        for first in (0, 4):
+        for first in (0, 2, 4, 6):
             peer_values(it, first)
-            for n, target in list(enumerate(zpeers))[first : first + 4]:
+            for n, target in list(enumerate(zpeers))[first : first + 2]:
                 to_peers([target], back_send.at[it, n], back_recv.at[it], z, back_ss.at[it], back_rs.at[it], True)
         sends.append((back_recv.at[it], len(zpeers), back_ss.at[it]))
         if last:
@@ -465,6 +478,9 @@
             blk_send[...] = block
             to_peers(ypeers, blk_send, blk_recv, y, blk_ss, blk_rs)
             blk_recv[y] = block
+        if not last:
+            arrived(other, early, epair_rs)
+            owner_kept(0, 5)
         arrived(zpeers, back_recv.at[it], back_rs.at[it])
         mine = both_tiles(
             lambda rows: tree_sum([back_send[it, NZ - 1, rows, :]] + [back_recv[it, pslot, rows, :] for _, _, pslot in zpeers])
@@ -472,44 +488,52 @@
         at_batch = tuple(damped(kt, t) for kt, t in enumerate(unpacked(*mine)))
         hist_at = hist_sm[it]
 
-        def density_step(group, carry):
-            at_tiles, acc = carry
-            rows = pl.ds(pl.multiple_of(group * 8, 8), 8)
+        accs = []
+        for group in range(batches // 4):
+            rows = pl.ds(group * 8, 8)
+            spread = [[jnp.broadcast_to(t[:, u : u + 1], (8, LANES)) for t in at_batch] for u in range(group * 4, group * 4 + 4)]
             parts = []
-            for u in range(4):
-                spread = [jnp.broadcast_to(t[:, u : u + 1], (8, LANES)) for t in at_tiles]
-                for half in range(2):
-                    at = group * 8 + u * 2 + half
-                    v = column * (tile_at(rho, at) + BETA * tile_at(res, at))
-                    parts.append(v - tree_sum([basis_tile(kt, at) * spread[kt] for kt in range(4)]))
+            for n in range(8):
+                at = group * 8 + n
+                v = column * (tile_at(rho, at) + BETA * tile_at(res, at))
+                parts.append(v - tree_sum([basis_tile(kt, at) * spread[n // 2][kt] for kt in range(4)]))
             dens = merge_all(parts, 1, 0)
             if last:
                 dens_out[rows, :] = dens
             else:
                 new = tgt[rows, :] + cpl[rows, :] * jnp.tanh(dens) - dens
                 fresh[rows, :] = new
+                mixed[rows, :] = dens
                 weighed = new * w[rows, :]
-                for u in range(8):
-                    cols = pl.ds(pl.multiple_of((group * 8 + u) * LANES, LANES), LANES)
-                    r = jnp.where(sub == hist_at, jnp.broadcast_to(new[u : u + 1], (8, LANES)), res[:, cols])
-                    res[:, cols] = r
-                    rho[:, cols] = jnp.where(sub == hist_at, jnp.broadcast_to(dens[u : u + 1], (8, LANES)), rho[:, cols])
-                    acc = acc + r * jnp.broadcast_to(weighed[u : u + 1], (8, LANES))
-            return tuple(pltpu.roll(t, LANES - 4, 1) for t in at_tiles), acc
-
-        _, acc = lax.fori_loop(0, batches // 4, density_step, (at_batch, jnp.zeros((8, LANES), F32)), unroll=4)
+                for n in range(8):
+                    r = jnp.where(
+                        sub == hist_at, jnp.broadcast_to(new[n : n + 1], (8, LANES)), tile_at(res, group * 8 + n)
+                    )
+                    accs.append(r * jnp.broadcast_to(weighed[n : n + 1], (8, LANES)))
+                accs = [tree_sum(accs)]
+
         if not last:
-            mine_new = jnp.broadcast_to(jnp.sum(acc, axis=1, keepdims=True), (8, LANES))
+            mine_new = jnp.broadcast_to(jnp.sum(accs[0], axis=1, keepdims=True), (8, LANES))
             columns = [
                 jnp.where(sub == hist_at, pltpu.roll(mine_new, d, 0) if d else mine_new, mine_new) for d in range(5)
             ]
             all_summed(row_of(columns), it + 1)
             send_raw(it + 1, fresh_moments())
+
+            def replace(step_at, carry):
+                for n in range(8):
+                    at = step_at * 8 + n
+                    cols = pl.ds(pl.multiple_of(at * LANES, LANES), LANES)
+                    res[:, cols] = jnp.where(sub == hist_at, row_at(fresh, at), res[:, cols])
+                    rho[:, cols] = jnp.where(sub == hist_at, row_at(mixed, at), rho[:, cols])
+                return carry
+
+            lax.fori_loop(0, tiles // 8, replace, 0)
+            plane_sum(it + 1)
             arrived(alike, kept.at[0], keep_rs)
             to_peers(other, kept.at[c], kept, c, pair_ss, pair_rs)
-            plane_sum(it + 1)
             arrived(other, kept, pair_rs)
-            owner_kept()
+            owner_kept(5, 6)
             arrived(peers, raw_recv.at[it + 1], raw_rs.at[it + 1])
             owner_fresh(it + 1)
             row_i = lane % 8
@@ -542,7 +566,7 @@
         scratch_shapes=[
             vm((tiles, LANES), F32), vm((tiles, LANES), F32), vm((tiles, LANES), F32),
             vm((LM, points), F32), vm((H, points), F32), vm((H, points), F32),
-            vm((tiles, LANES), F32), vm((16, 4, 8, LANES), F32), vm((batches // 8, 25, 8, LANES), F32), vm((25, 8, LANES), F32),
+            vm((tiles, LANES), F32), vm((tiles, LANES), F32), vm((16, 4, 8, LANES), F32), vm((batches // 8, 25, 8, LANES), F32), vm((25, 8, LANES), F32),
             sm((batches,), I32), sm((slots,), I32), sm((ITERS,), I32),
             vm((1, LANES), I32), vm((PLANE, 1, LANES), I32), vm((NZ, 1, LANES), I32),
             vm((ITERS, 1, LANES), F32), vm((ITERS, PLANE, 1, LANES), F32),
@@ -551,12 +575,13 @@
             vm((LM, LANES), F32), vm((NZ, LM, LANES), F32),
             vm((ITERS, NZ, 13, LANES), F32), vm((ITERS, NZ, 13, LANES), F32),
             vm((LM, LANES), F32), vm((NY, LM, LANES), F32),
-            vm((88, LANES), F32), vm((NC, NY * NX, 88, LANES), F32),
+            vm((40, LANES), F32), vm((NC, NY * NX, 40, LANES), F32), vm((48, LANES), F32), vm((NC, NY * NX, 48, LANES), F32),
             vm((NZ * 64 + LANES, PLANE * 64), jnp.bfloat16), vm((96, PLANE * 64), jnp.bfloat16),
-            vm((528, PLANE * 64), jnp.bfloat16), vm((176, LANES), F32), vm((32, LANES), F32),
+            vm((288, PLANE * 64), jnp.bfloat16), vm((176, LANES), F32), vm((32, LANES), F32),
             dma((9,)),
             dma, dma, dma, dma, dma((ITERS,)), dma((ITERS,)), dma((ITERS,)), dma((ITERS,)),
             dma((ITERS,)), dma((ITERS,)), dma, dma, dma((ITERS,)), dma((ITERS,)), dma, dma, dma, dma, dma, dma,
+            dma, dma, dma, dma,
         ],
         compiler_params=pltpu.CompilerParams(collective_id=0, has_side_effects=True),
     )(

time: 50.7 us -> 49.1 us (0.968)
  Pallas kernels: 48.7 us -> 47.1 us
    pallas_call x1, Pallas kernels: 48.7 us -> 47.1 us  [local(): pl.pallas_call(functools.partial(kernel, tiles, batches, scale), out_shap...]
where the time goes in v6:
time: 49.1 us; the launch traced here: 49 us
  Pallas kernels  47.1 us (96%)
  local copies, waits for them, and re-layouts  1.26 us (3%)
  between operations  0.64 us (1%)
    pallas_call x1, Pallas kernels, local(): pl.pallas_call(functools.partial(kernel, tiles, batches, scale), out_shap...  47.1 us
    unnamed x2, local copies, waits for them, and re-layouts  1.26 us

profile of v6, /device:TPU:2, one launch (start us, length us, event | category | flops | bytes accessed | tf_op | source)
XLA Modules:
  0.0 49.0 jit_solution(11511593062453035160)
XLA Ops:
  0.6 47.1 %shard_map.104 = (f32[128,128]{1,0:T(8,128)S(1)}, f32[25,512]{1,0:T(8,128)S(1)}) custom-call(f32[128,128]{1,0:T(8,128)} %bitcast.5, f32[128,128]{1,0:T(8,128)} %bitcast.6, f32[128,128]{1,0:T(8,128)} %bitcast.7, f32[25,16384]{1,0:T(8,128)} %basis_hbm.1, f32[8,16384]{1,0:T(8,128)} %rho_hbm.1, f32[8,16384]{1,0:T(8,128)} %res_hbm.1, s32[64]{0:T(128)} %atom_hbm.1, ...), custom_call_target="tpu_custom_call" | custom-call | tf_op jit(solution)/shard_map/pallas_call | solution.py:561
  47.7 0.6 %copy.13 = f32[16384]{0:T(1024)} copy(f32[16384]{0:T(1024)S(1)} %bitcast.4) | data formatting | bytes 131072
  48.3 0.6 %copy.14 = f32[25,512]{1,0:T(8,128)} copy(f32[25,512]{1,0:T(8,128)S(1)} %get-tuple-element.7) | data formatting | bytes 102400

commit v7 on v6

--- a/solution.py
+++ b/solution.py
@@ -44,21 +44,19 @@
 
     ys = [(y + d) % NY for d in range(NY)]
     xs = [(x + d) % NX for d in range(NX)]
-    cs = [c, 1 - c]
     peers = []
     for dy in (2, 1, 3, 0):
         for dx in (2, 1, 3, 0):
-            for dc in (1, 0):
-                if dy or dx or dc:
-                    pa = xs[dx] * NC + cs[dc]
-                    peers.append((z * NY + ys[dy], pa, ys[dy] * (NX * NC) + pa))
+            for core in (0, 1) if dy or dx else (1 - c,):
+                pa = xs[dx] * NC + core
+                peers.append((z * NY + ys[dy], pa, ys[dy] * (NX * NC) + pa))
     zpeers = []
     zorder = [(z + dz) % NZ for dz in (4, 3, 5, 2, 6, 1, 7, 0)]
     for pz in zorder[:-1]:
         zpeers.append((pz * NY + y, atom, pz))
     spot = y * NX + x
     alike = [(pg, xs[dx] * NC + c, 0) for dy in (2, 1, 3, 0) for dx in (2, 1, 3, 0) if dy or dx for pg in [z * NY + ys[dy]]]
-    other = [(grid, x * NC + cs[1], 0)]
+    other = [(grid, x * NC + 1 - c, 0)]
     ypeers = [(z * NY + ys[dy], atom, ys[dy]) for dy in (2, 1, 3)]
 
     barrier = pltpu.get_barrier_semaphore()
@@ -588,6 +586,20 @@
         square(weights), square(target), square(coupling), multipole_basis, rho_hist, res_hist,
         batch_atom, owner_slot, slot_index,
     )
+    def finish(d_in, m_in, d_out, m_out, sem):
+        copies = [pltpu.make_async_copy(d_in, d_out, sem.at[0]), pltpu.make_async_copy(m_in, m_out, sem.at[1])]
+        for copy in copies:
+            copy.start()
+        for copy in copies:
+            copy.wait()
+
+    density, moments = pl.pallas_call(
+        finish,
+        out_shape=(jax.ShapeDtypeStruct((tiles, LANES), F32), jax.ShapeDtypeStruct((LM, owned), F32)),
+        in_specs=[vmem] * 2,
+        out_specs=(anywhere, anywhere),
+        scratch_shapes=[dma((2,))],
+    )(pltpu.with_memory_space_constraint(density, pltpu.VMEM), pltpu.with_memory_space_constraint(moments, pltpu.VMEM))
     return density.reshape(points), moments
 
 

time: 49.1 us -> 48.5 us (0.988)
  local copies, waits for them, and re-layouts: 1.26 us -> 0 us
  Pallas kernels: 47.1 us -> 47.8 us
    unnamed x2 -> x0, local copies, waits for them, and re-layouts: 1.26 us -> none
    pallas_call x0 -> x1, Pallas kernels: none -> 0.67 us  [local(): pl.pallas_call(finish, out_shape=(jax.ShapeDtypeStruct((tiles, LANES), F3...]
where the time goes in v7:
time: 48.5 us; the launch traced here: 48.4 us
  Pallas kernels  47.8 us (99%)
  between operations  0.64 us (1%)
    pallas_call x1, Pallas kernels, local(): pl.pallas_call(functools.partial(kernel, tiles, batches, scale), out_shap...  47.1 us

profile of v7, /device:TPU:2, one launch (start us, length us, event | category | flops | bytes accessed | tf_op | source)
XLA Modules:
  0.0 48.4 jit_solution(3502457332936174776)
XLA Ops:
  0.6 47.1 %shard_map.104 = (f32[128,128]{1,0:T(8,128)S(1)}, f32[25,512]{1,0:T(8,128)S(1)}) custom-call(f32[128,128]{1,0:T(8,128)} %bitcast.4, f32[128,128]{1,0:T(8,128)} %bitcast.5, f32[128,128]{1,0:T(8,128)} %bitcast.6, f32[25,16384]{1,0:T(8,128)} %basis_hbm.1, f32[8,16384]{1,0:T(8,128)} %rho_hbm.1, f32[8,16384]{1,0:T(8,128)} %res_hbm.1, s32[64]{0:T(128)} %atom_hbm.1, ...), custom_call_target="tpu_custom_call" | custom-call | tf_op jit(solution)/shard_map/pallas_call | solution.py:559
  47.7 0.7 %shard_map.105 = (f32[128,128]{1,0:T(8,128)}, f32[25,512]{1,0:T(8,128)}) custom-call(f32[128,128]{1,0:T(8,128)S(1)} %get-tuple-element.6.d_in, f32[25,512]{1,0:T(8,128)S(1)} %get-tuple-element.7.m_in), custom_call_target="tpu_custom_call" | custom-call | tf_op jit(solution)/shard_map/pallas_call | solution.py:596

commit v8 on v7

--- a/solution.py
+++ b/solution.py
@@ -60,7 +60,7 @@
     ypeers = [(z * NY + ys[dy], atom, ys[dy]) for dy in (2, 1, 3)]
 
     barrier = pltpu.get_barrier_semaphore()
-    for pg, pa, _ in peers + zpeers:
+    for pg, pa, _ in zpeers[:3] + peers + zpeers[3:]:
         pl.semaphore_signal(barrier, inc=1, device_id=(pg, pa), device_id_type=MESH)
 
     loads = [
@@ -518,6 +518,7 @@
             all_summed(row_of(columns), it + 1)
             send_raw(it + 1, fresh_moments())
 
+            plane_sum(it + 1)
             def replace(step_at, carry):
                 for n in range(8):
                     at = step_at * 8 + n
@@ -527,7 +528,6 @@
                 return carry
 
             lax.fori_loop(0, tiles // 8, replace, 0)
-            plane_sum(it + 1)
             arrived(alike, kept.at[0], keep_rs)
             to_peers(other, kept.at[c], kept, c, pair_ss, pair_rs)
             arrived(other, kept, pair_rs)

time: 48.5 us -> 48.3 us (level)
  no operation moved by 1% of the time
where the time goes in v8:
time: 48.3 us; the launch traced here: 48.2 us
  Pallas kernels  47.6 us (99%)
  between operations  0.64 us (1%)
    pallas_call x1, Pallas kernels, local(): pl.pallas_call(functools.partial(kernel, tiles, batches, scale), out_shap...  46.9 us

profile of v8, /device:TPU:2, one launch (start us, length us, event | category | flops | bytes accessed | tf_op | source)
XLA Modules:
  0.0 48.2 jit_solution(6310939259352631803)
XLA Ops:
  0.6 46.9 %shard_map.104 = (f32[128,128]{1,0:T(8,128)S(1)}, f32[25,512]{1,0:T(8,128)S(1)}) custom-call(f32[128,128]{1,0:T(8,128)} %bitcast.4, f32[128,128]{1,0:T(8,128)} %bitcast.5, f32[128,128]{1,0:T(8,128)} %bitcast.6, f32[25,16384]{1,0:T(8,128)} %basis_hbm.1, f32[8,16384]{1,0:T(8,128)} %rho_hbm.1, f32[8,16384]{1,0:T(8,128)} %res_hbm.1, s32[64]{0:T(128)} %atom_hbm.1, ...), custom_call_target="tpu_custom_call" | custom-call | tf_op jit(solution)/shard_map/pallas_call | solution.py:559
  47.5 0.7 %shard_map.105 = (f32[128,128]{1,0:T(8,128)}, f32[25,512]{1,0:T(8,128)}) custom-call(f32[128,128]{1,0:T(8,128)S(1)} %get-tuple-element.6.d_in, f32[25,512]{1,0:T(8,128)S(1)} %get-tuple-element.7.m_in), custom_call_target="tpu_custom_call" | custom-call | tf_op jit(solution)/shard_map/pallas_call | solution.py:596
